TPU v7x, 128 devices: a whole 4x4x4 slice. The times are simulated.
128 devices in a mesh: section: 2 (over core), tp: 4 (over x), pool: 16 (over z, y).
Axes of the slice: x: 4, y: 4, z: 4, core: 2. Of those that a mesh axis runs over, the one named last changes fastest.
Arguments:
- hidden: bfloat16 [2, 16, 128, 8192], P('section', 'pool', None, 'tp'), may hold values from -6 to 6
- queries: bfloat16 [2, 16, 16, 8, 64, 128], P('section', 'pool', None, None, 'tp'), may hold values from -450 to 450, as said below
- window_key_value: bfloat16 [2, 16, 16, 2, 8, 8, 128], P('section', 'pool', None, None, 'tp'), may hold values from -12 to 12
- cached_key_value: bfloat16 [2, 16, 128, 2, 8, 64, 128], P('section', 'pool', None, None, 'tp'), may hold values from -12 to 12
- cached_length: int32 [2, 16, 16], P('section', 'pool'), may hold values from 1 to 1024, 6144 in all within a row
- request_page_table: int32 [2, 16, 16, 16], P('section', 'pool'), may hold values from 0 to 127
- request_adapter: int32 [2, 16, 16], replicated, may hold values from 0 to 127, as said below
- layer_page_slot: int32 [256], replicated, may hold values from 0 to 255, as said below
- wo: bfloat16 [2, 8192, 8192], P('section', 'tp'), may hold values from -0.09375 to 0.09375
- adapter_down: bfloat16 [256, 64, 8192], P(('section', 'pool'), None, 'tp'), may hold values from -0.0625 to 0.0625
- adapter_up: bfloat16 [256, 64, 8192], P(('section', 'pool'), None, 'tp'), may hold values from -0.75 to 0.75
Outputs:
- next_hidden: bfloat16 [2, 16, 128, 8192], P('section', 'pool', None, 'tp')
Inputs may be any that keep to these rules, and one draw needn't show every extreme that they name: `queries`: queries of order one; some entries far larger in the hidden draw. `request_page_table`: several requests may name the same cache page; entries past a request's length are read but excluded. `cached_length`: each request of a device has 1 to 1024 cached positions. `layer_page_slot`: the adapters of layer s occupy slots s * 128 to (s + 1) * 128 - 1, each slot once; slot q lies on the index q // 8 of section and pool taken together, section first, so layer s's pages sit on section s. `request_adapter`: up to all 16 requests of a pool group may use adapters held on one pool index, and one pool index may serve every request of its section.
All inputs are finite; a program needn't handle non-finite values.
Results may differ from a plain program's by a relative error of at most 0.009.
Values may be sent and summed in bfloat16 or wider, within the bound.
A program may use at most 192 MiB of HBM per device.

v0:
```python
import jax
import jax.numpy as jnp
from jax import lax
from jax.sharding import PartitionSpec as P


def from_behind(value, axis, steps):
    count = lax.axis_size(axis)
    pairs = [(source, (source + steps) % count) for source in range(count)]
    return lax.ppermute(value, axis, pairs)


def attend(queries, cache_pages, window_kv, lengths, page_rows):
    requests, window, head_count, head_size = queries.shape
    kv_heads = window_kv.shape[2]
    page_tok = cache_pages.shape[3]
    max_pages = page_rows.shape[1]
    cached = max_pages * page_tok
    picked = jnp.take(cache_pages, page_rows, axis=0)
    picked = jnp.transpose(picked, (0, 2, 3, 1, 4, 5)).reshape(
        requests, 2, kv_heads, cached, head_size
    )
    keys_all = jnp.concatenate([picked, window_kv], axis=3)
    grouped = queries.reshape(requests, window, kv_heads, head_count // kv_heads, head_size)
    scores = jnp.einsum(
        "rwkgd,rktd->rkgwt", grouped, keys_all[:, 0], preferred_element_type=jnp.float32
    ) * head_size ** (-0.5)
    position = jnp.arange(cached + window, dtype=jnp.int32)
    query_pos = jnp.arange(window, dtype=jnp.int32)
    in_cache = position[None, :] < lengths[:, None]
    in_window = (position[None, :] >= cached) & (position[None, :] - cached <= query_pos[:, None])
    allowed = in_cache[:, None, :] | in_window[None, :, :]
    scores = jnp.where(allowed[:, None, None, :, :], scores, -jnp.inf)
    largest = jnp.max(scores, axis=-1, keepdims=True)
    weights = jnp.exp(scores - largest)
    probs = (weights / jnp.sum(weights, axis=-1, keepdims=True)).astype(jnp.bfloat16)
    context = jnp.einsum(
        "rkgwt,rktd->rwkgd", probs, keys_all[:, 1], preferred_element_type=jnp.float32
    )
    return context.reshape(requests, window, head_count * head_size).astype(jnp.bfloat16)


def per_device(
    hidden,
    queries,
    window_key_value,
    cached_key_value,
    cached_length,
    request_page_table,
    request_adapter,
    layer_page_slot,
    wo,
    adapter_down,
    adapter_up,
):
    section_count = lax.axis_size("section")
    section_index = lax.axis_index("section")
    pool_index = lax.axis_index("pool")
    context = attend(
        queries[0, 0],
        cached_key_value[0, 0],
        window_key_value[0, 0],
        cached_length[0, 0],
        request_page_table[0, 0],
    )
    requests, window, width_of_head = context.shape
    flat_rows = context.reshape(requests * window, width_of_head)
    partial_out = jnp.dot(flat_rows, wo[0], preferred_element_type=jnp.float32)
    plain_output = lax.psum_scatter(partial_out, "tp", scatter_dimension=1, tiled=True)
    pages_per_member = adapter_down.shape[0]
    rank_width = adapter_down.shape[1]
    output_width = adapter_up.shape[2]
    adapters = layer_page_slot.shape[0] // section_count
    layer_start = section_index * adapters
    everyone = lax.all_gather(context, "pool", axis=0, tiled=True)
    total_requests = everyone.shape[0]
    all_slots = layer_page_slot[layer_start + request_adapter[section_index]].reshape(
        total_requests
    )
    local_slot = all_slots - layer_start - pool_index * pages_per_member
    owned_mask = (
        local_slot[:, None] == jnp.arange(pages_per_member, dtype=jnp.int32)[None, :]
    ).astype(jnp.float32)
    stacked_down = adapter_down.reshape(pages_per_member * rank_width, width_of_head)
    wide_rank = lax.dot_general(
        everyone, stacked_down, (((2,), (1,)), ((), ())), preferred_element_type=jnp.float32
    )
    wide_rank = wide_rank.reshape(total_requests, window, pages_per_member, rank_width)
    rank_hidden = jnp.sum(wide_rank * owned_mask[:, None, :, None], axis=2)
    rank_hidden = lax.psum(rank_hidden, "tp")
    broadcast_rows = (
        rank_hidden.astype(jnp.bfloat16)[:, :, None, :]
        * owned_mask.astype(jnp.bfloat16)[:, None, :, None]
    )
    broadcast_rows = broadcast_rows.reshape(total_requests * window, pages_per_member * rank_width)
    product = jnp.dot(
        broadcast_rows,
        adapter_up.reshape(pages_per_member * rank_width, output_width),
        preferred_element_type=jnp.float32,
    )
    returned = lax.all_to_all(
        product.astype(jnp.bfloat16), "pool", split_axis=0, concat_axis=0, tiled=True
    )
    adapter_delta = jnp.sum(
        returned.reshape(-1, requests * window, output_width).astype(jnp.float32), axis=0
    )
    blended_output = (hidden[0, 0].astype(jnp.float32) + plain_output + adapter_delta).astype(
        jnp.bfloat16
    )
    handed = from_behind(blended_output, "section", 1)
    return handed[None, None]


def solution(mesh):
    return jax.shard_map(
        per_device,
        mesh=mesh,
        in_specs=(
            P("section", "pool", None, "tp"),
            P("section", "pool", None, None, "tp", None),
            P("section", "pool", None, None, "tp", None, None),
            P("section", "pool", None, None, "tp", None, None),
            P("section", "pool", None),
            P("section", "pool", None, None),
            P(),
            P(),
            P("section", "tp", None),
            P(("section", "pool"), None, "tp"),
            P(("section", "pool"), None, "tp"),
        ),
        out_specs=P("section", "pool", None, "tp"),
        check_vma=False,
    )
```

profile of v0, /device:TPU:1, one launch (start us, length us, event | category | flops | bytes accessed | tf_op | source)
XLA Modules:
  0.0 319.3 jit_solution(6340486119828184799)
XLA Ops:
  7.4 0.0 copy-start
  7.4 0.0 all-gather.2.cloned.1.call-start
  7.4 0.8 compare_select_fusion.1
  8.2 0.7 compare_and_fusion
  8.9 0.1 reshape.214
  9.0 0.9 copy.45
  9.9 0.7 iota_compare_fusion
  10.7 13.1 %gather_fusion = bf16[256,2,2,64,128]{4,3,2,1,0:T(8,128)(2,1)} fusion(bf16[128,2,2,64,128]{4,3,2,1,0:T(8,128)(2,1)} %bitcast.82, s32[1024]{0:T(1024)S(1)} %pad_clamp_fusion.1), kind=kCustom, calls=%fused_computation | custom fusion | bytes 33555456 | tf_op jit(solution)/shard_map/jit(_take)/gather | solution.py:19
  23.8 0.0 copy-start.3
  23.8 14.2 %copy_select_fusion = bf16[16,16,2,2,64,128]{5,4,1,3,0,2:T(8,128)(2,1)} fusion(bf16[16,16,2,2,64,128]{5,4,3,2,1,0:T(8,128)(2,1)} %bitcast.81, pred[16,16]{1,0:T(8,128)(4,1)S(1)} %compare_and_fusion), kind=kLoop, calls=%fused_computation.7 | loop fusion | flops 8388608 | bytes 33554688 | tf_op jit(solution)/shard_map/jit(_take)/select_n | solution.py:19
  38.0 0.1 broadcast_or_fusion
  38.1 0.0 copy-done.3
  38.1 8.2 %fusion.36 = (f32[16,2,8,8]{2,3,1,0:T(8,128)S(1)}, f32[16,2,8,8,1032]{4,2,3,1,0:T(8,128)}) fusion(pred[16,8,1032]{2,1,0:T(8,128)(4,1)S(1)} %broadcast_or_fusion, bf16[16,2,2,8,128]{4,3,2,0,1:T(8,128)(2,1)S(1)} %bitcast.89, bf16[16,2,2,1024,128]{4,3,2,0,1:T(8,128)(2,1)} %bitcast.83, bf16[1,1,16,8,16,128]{5,4,3,2,1,0:T(8,128)(2,1)S(1)} %copy-done.3), kind=kOutput, calls=%fused_computation.56 | convolution fusion | flops 566428672 | bytes 26027008 | tf_op jit(solution)/shard_map/sub | solution.py:35
  46.3 7.1 %divide_convert_fusion = bf16[16,2,8,8,1032]{4,2,3,1,0:T(8,128)(2,1)} fusion(f32[16,2,8,8,1032]{4,2,3,1,0:T(8,128)} %get-tuple-element.8, f32[16,2,8,8]{2,3,1,0:T(8,128)S(1)} %get-tuple-element.7), kind=kLoop, calls=%fused_computation.10 | loop fusion | flops 4227072 | bytes 12689408 | tf_op jit(solution)/shard_map/convert_element_type | solution.py:36
  53.4 0.0 copy-start.2
  53.4 0.0 copy-start.1
  53.4 6.3 %fusion.21 = bf16[16,2,128,8,8]{2,4,3,1,0:T(8,128)(2,1)S(1)} fusion(bf16[16,2,8,8,1032]{4,2,3,1,0:T(8,128)(2,1)} %divide_convert_fusion, bf16[16,2,2,1024,128]{4,3,2,0,1:T(8,128)(2,1)} %bitcast.84, bf16[16,2,2,8,128]{4,3,2,0,1:T(8,128)(2,1)S(1)} %bitcast.90), kind=kOutput, calls=%fused_computation.30 | convolution fusion | flops 558235648 | bytes 21659648 | tf_op jit(solution)/shard_map/rkgwt,rktd->rwkgd/dot_general | solution.py:37
  59.7 1.1 copy.27
  60.8 0.0 all-gather.2.cloned.1.call-update
  60.8 0.0 copy-done.2
  60.8 0.1 reshape.222
  60.9 0.0 copy-done.1
  60.9 1.9 gather_fusion.1
  62.9 0.1 copy.29
  63.1 71.9 %all-gather.2.cloned.1.call-done = bf16[256,8,2048]{2,0,1:T(8,128)(2,1)} async-done(((bf16[16,8,2048]{2,0,1:T(8,128)(2,1)}), bf16[256,8,2048]{2,0,1:T(8,128)(2,1)}) %all-gather.2.cloned.1.call-update) | async-done | bytes 8388624 | tf_op jit(solution)/shard_map/all_gather | solution.py:75
  134.9 8.5 %multiply_reduce_fusion = f32[256,8,64]{0,2,1:T(8,128)S(1)} fusion(bf16[256,8,2048]{2,0,1:T(8,128)(2,1)} %all-gather.2.cloned.1.call-done, bf16[8,64,2048]{2,1,0:T(8,128)(2,1)} %param.20, f32[256,8]{0,1:T(8,128)S(1)} %get-tuple-element.5), kind=kOutput, calls=%fused_computation.27 | convolution fusion | flops 4296933376 | bytes 11018240 | tf_op jit(solution)/shard_map/dot_general | solution.py:85
  143.5 18.2 %all-reduce.1 = bf16[256,8,64]{0,2,1:T(8,128)(2,1)S(1)} all-reduce(f32[256,8,64]{0,2,1:T(8,128)S(1)} %multiply_reduce_fusion), channel_id=1, replica_groups=mesh['section'=2,'tp'=4,'pool'=16] {'tp'}, use_global_device_ids=true, to_apply=%region_4.5 | all-reduce | flops 131072 | bytes 786432 | tf_op jit(solution)/shard_map/psum | solution.py:90
  161.7 0.3 copy.28
  162.0 2.3 broadcast_multiply_fusion
  164.3 6.5 %mul.56 = bf16[2048,512]{1,0:T(8,128)(2,1)} reshape(bf16[256,8,8,64]{3,2,1,0:T(8,128)(2,1)} %broadcast_multiply_fusion) | data formatting | bytes 4194304 | tf_op jit(solution)/shard_map/mul | solution.py:92
  170.8 0.0 copy-done
  170.8 8.4 %convolution_convert_fusion = bf16[2048,2048]{1,0:T(8,128)(2,1)} fusion(bf16[2048,512]{1,0:T(8,128)(2,1)} %mul.56, bf16[512,2048]{1,0:T(8,128)(2,1)S(1)} %bitcast.80), kind=kOutput, calls=%fused_computation.22 | convolution fusion | flops 4299161600 | bytes 12582912 | tf_op jit(solution)/shard_map/dot_general | solution.py:96
  179.2 5.1 %all-to-all-start = ((bf16[16,128,2048]{2,1,0:T(8,128)(2,1)}), bf16[16,128,2048]{2,1,0:T(8,128)(2,1)}, u32[]{:S(2)}, u32[]{:S(2)}) async-start(bf16[16,128,2048]{2,1,0:T(8,128)(2,1)} %bitcast.85), calls=%async_computation.1 | async-start | bytes 16777216 | tf_op jit(solution)/shard_map/all_to_all | solution.py:101
  184.3 0.0 reduce-scatter.2.cloned.1.call-start
  184.3 17.0 %fusion.1 = f32[128,8192]{1,0:T(8,128)} fusion(bf16[128,2048]{1,0:T(8,128)(2,1)S(1)} %bitcast.87, bf16[1,2048,8192]{2,1,0:T(8,128)(2,1)} %param.19), kind=kOutput, calls=%fused_computation.3 | convolution fusion | flops 4294967296 | bytes 38273024 | tf_op jit(solution)/shard_map/dot_general | solution.py:68
  201.3 0.0 reduce-scatter.2.cloned.1.call-update
  201.3 94.3 %all-to-all-done = bf16[16,128,2048]{2,1,0:T(8,128)(2,1)} async-done(((bf16[16,128,2048]{2,1,0:T(8,128)(2,1)}), bf16[16,128,2048]{2,1,0:T(8,128)(2,1)}, u32[]{:S(2)}, u32[]{:S(2)}) %all-to-all-start) | async-done | bytes 8388640 | tf_op jit(solution)/shard_map/all_to_all | solution.py:101
  295.7 5.3 %convert_reduce_fusion = f32[128,2048]{1,0:T(8,128)S(1)} fusion(bf16[16,128,2048]{2,1,0:T(8,128)(2,1)} %all-to-all-done), kind=kLoop, calls=%fused_computation.8 | loop fusion | flops 8126464 | bytes 9437184 | tf_op jit(solution)/shard_map/reduce_sum | solution.py:104
  301.0 0.0 reduce-scatter.2.cloned.1.call-done
  301.0 1.5 fusion.27
  302.5 7.0 %collective-permute-start = (bf16[128,2048]{1,0:T(8,128)(2,1)S(1)}, bf16[128,2048]{1,0:T(8,128)(2,1)S(1)}, u32[]{:S(2)}, u32[]{:S(2)}) collective-permute-start(bf16[128,2048]{1,0:T(8,128)(2,1)S(1)} %fusion.27), channel_id=1, source_target_pairs={{0,64},{64,0},{1,65},{65,1},{2,66},{66,2},{3,67},{67,3},{4,68},{68... | collective-permute-start | bytes 1572872 | tf_op jit(solution)/shard_map/ppermute | solution.py:10
  309.5 1.5 collective-permute-done
  311.1 0.8 copy.49
  (8 shorter events, 0.1 us)
Async XLA Ops:
  7.4 163.5 %copy-start = (bf16[8,64,2048]{2,1,0:T(8,128)(2,1)S(1)}, bf16[8,64,2048]{2,1,0:T(8,128)(2,1)}, u32[]{:S(2)}) copy-start(bf16[8,64,2048]{2,1,0:T(8,128)(2,1)} %param.21) | copy-start | bytes 6291460
  7.4 127.6 %all-gather.2.cloned.1.call-start = ((), (), s32[]{:S(2)}) async-start(), calls=%async_computation.3 | async-start | bytes 8912896 | tf_op jit(solution)/shard_map/all_gather | solution.py:75
  23.8 14.3 %copy-start.3 = (bf16[1,1,16,8,16,128]{5,4,3,2,1,0:T(8,128)(2,1)S(1)}, bf16[1,1,16,8,16,128]{5,4,3,2,1,0:T(8,128)(2,1)}, u32[]{:S(2)}) copy-start(bf16[1,1,16,8,16,128]{5,4,3,2,1,0:T(8,128)(2,1)} %param.12) | copy-start | bytes 1572868
  53.4 7.4 %copy-start.2 = (s32[2,16,16]{2,1,0:T(8,128)S(1)}, s32[2,16,16]{2,1,0:T(8,128)}, u32[]{:S(2)}) copy-start(s32[2,16,16]{2,1,0:T(8,128)} %param.17) | copy-start | bytes 6148
  53.4 7.5 %copy-start.1 = (s32[256]{0:T(256)S(1)}, s32[256]{0:T(256)}, u32[]{:S(2)}) copy-start(s32[256]{0:T(256)} %param.18) | copy-start | bytes 3076
  179.2 116.5 %all-to-all-start = ((bf16[16,128,2048]{2,1,0:T(8,128)(2,1)}), bf16[16,128,2048]{2,1,0:T(8,128)(2,1)}, u32[]{:S(2)}, u32[]{:S(2)}) async-start(bf16[16,128,2048]{2,1,0:T(8,128)(2,1)} %bitcast.85), calls=%async_computation.1 | async-start | bytes 16777216 | tf_op jit(solution)/shard_map/all_to_all | solution.py:101
  184.3 116.7 %reduce-scatter.2.cloned.1.call-start = ((), (), s32[]{:S(2)}) async-start(), calls=%async_computation.2 | async-start | bytes 5242880 | tf_op jit(solution)/shard_map/reduce_scatter | solution.py:69
  302.5 8.5 %collective-permute-start = (bf16[128,2048]{1,0:T(8,128)(2,1)S(1)}, bf16[128,2048]{1,0:T(8,128)(2,1)S(1)}, u32[]{:S(2)}, u32[]{:S(2)}) collective-permute-start(bf16[128,2048]{1,0:T(8,128)(2,1)S(1)} %fusion.27), channel_id=1, source_target_pairs={{0,64},{64,0},{1,65},{65,1},{2,66},{66,2},{3,67},{67,3},{4,68},{68... | collective-permute-start | bytes 1572872 | tf_op jit(solution)/shard_map/ppermute | solution.py:10
Sparse Core Ops, SparseCore 0:
  60.9 73.9 all-gather.1
Sparse Core Ops, SparseCore 1:
  201.4 51.6 reduce-scatter.1
where the time goes:
time: 321 us; the launch traced here: 319 us
  waiting for transfers between devices  168 us (52%)
  matrix products  48.3 us (15%)
  other arithmetic  32.9 us (10%)
  local copies, waits for them, and re-layouts  25 us (8%)
  blocking collectives  18.2 us (6%)
  between operations  15 us (5%)
  starting transfers between devices  12.1 us (4%)
    all_to_all x1, waiting for transfers between devices, per_device(): lax.all_to_all(product.astype(jnp.bfloat16), 'pool', split_axis=0, concat...  94.3 us
    all_gather x1, waiting for transfers between devices, per_device(): everyone = lax.all_gather(context, 'pool', axis=0, tiled=True)  71.9 us
    psum x1, blocking collectives, per_device(): rank_hidden = lax.psum(rank_hidden, 'tp')  18.2 us
    dot_general x1, matrix products, per_device(): partial_out = jnp.dot(flat_rows, wo[0], preferred_element_type=jnp.float32)  17 us
    select_n x2, other arithmetic, attend(): picked = jnp.take(cache_pages, page_rows, axis=0)  15 us
    gather x1, local copies, waits for them, and re-layouts, attend(): picked = jnp.take(cache_pages, page_rows, axis=0)  13.1 us
    dot_general x1, matrix products, per_device(): lax.dot_general(everyone, stacked_down, (((2,), (1,)), ((), ())), preferr...  8.55 us
    dot_general x1, matrix products, per_device(): jnp.dot(broadcast_rows, adapter_up.reshape(pages_per_member * rank_width,...  8.36 us
  transfers between devices with their start and end apart: 4, of which 3 were waited for; matrix products, arithmetic and copies ran while one was open for 8% of the time, Pallas kernels for 0%

commit v1 on v0

v1 whole, which is shorter than its diff:
```python
import functools

import jax
import jax.numpy as jnp
from jax import lax
from jax.experimental import pallas as pl
from jax.experimental.pallas import tpu as pltpu
from jax.sharding import PartitionSpec as P

F32 = jnp.float32
BF16 = jnp.bfloat16
VMEM = pltpu.VMEM
NT = (((1,), (1,)), ((), ()))
TN = (((0,), (0,)), ((), ()))


def vspec():
    return pl.BlockSpec(memory_space=pltpu.VMEM)


def sspec():
    return pl.BlockSpec(memory_space=pltpu.SMEM)


def aspec():
    return pl.BlockSpec(memory_space=pl.ANY)


BUCKETS = (4, 8, 16)


def attend_kernel(
    len_ref, table_ref, q_ref, wkv_ref, cache_ref, heads_ref, flat_ref, slot, ctx32, sems
):
    requests = q_ref.shape[0]
    page = cache_ref.shape[3]
    scale = q_ref.shape[3] ** (-0.5)

    def bucket(r, fn):
        length = len_ref[r]
        low = 0
        for pages in BUCKETS:
            high = pages * page

            @pl.when((length > low) & (length <= high))
            def _():
                fn(pages)

            low = high

    def fetch(r, carry):
        def start(pages):
            for j in range(pages):
                pltpu.make_async_copy(
                    cache_ref.at[table_ref[r, j]], slot.at[r, j], sems.at[r]
                ).start()

        bucket(r, start)
        return carry

    lax.fori_loop(0, requests, fetch, 0)

    def one(r, carry):
        length = len_ref[r]
        zero = jnp.zeros(q_ref.shape[2:], BF16)
        query = jnp.concatenate(
            [
                jnp.concatenate([q_ref[r, 0], zero], axis=1),
                jnp.concatenate([zero, q_ref[r, 1]], axis=1),
            ],
            axis=0,
        )
        window_key = jnp.concatenate([wkv_ref[r, 0, 0], wkv_ref[r, 0, 1]], axis=1)
        window_value = jnp.concatenate([wkv_ref[r, 1, 0], wkv_ref[r, 1, 1]], axis=1)

        def work(pages):
            pltpu.make_async_copy(
                cache_ref.at[0:pages], slot.at[r, 0:pages], sems.at[r]
            ).wait()
            count = pages * page

            def side(kv, head):
                return slot[r, 0:pages, kv, head].reshape(count, 128)

            keys = jnp.concatenate([side(0, 0), side(0, 1)], axis=1)
            values = jnp.concatenate([side(1, 0), side(1, 1)], axis=1)
            s = lax.dot_general(keys, query, NT, preferred_element_type=F32) * scale
            position = lax.broadcasted_iota(jnp.int32, s.shape, 0)
            s = jnp.where(position < length, s, -1e30)
            sw = lax.dot_general(window_key, query, NT, preferred_element_type=F32) * scale
            row = lax.broadcasted_iota(jnp.int32, sw.shape, 0)
            token = lax.broadcasted_iota(jnp.int32, sw.shape, 1) % 8
            sw = jnp.where(row <= token, sw, -1e30)
            top = jnp.maximum(
                jnp.max(s, axis=0, keepdims=True), jnp.max(sw, axis=0, keepdims=True)
            )
            p = jnp.exp(s - top)
            pw = jnp.exp(sw - top)
            total = jnp.sum(p, axis=0, keepdims=True) + jnp.sum(pw, axis=0, keepdims=True)
            inverse = 1.0 / total
            p = (p * inverse).astype(BF16)
            pw = (pw * inverse).astype(BF16)
            out = lax.dot_general(p, values, TN, preferred_element_type=F32)
            out = out + lax.dot_general(pw, window_value, TN, preferred_element_type=F32)
            rows = pl.ds(pl.multiple_of(r * 8, 8), 8)
            ctx32[0:8, rows, :] = out[0:64, 0:128].reshape(8, 8, 128)
            ctx32[8:16, rows, :] = out[64:128, 128:256].reshape(8, 8, 128)

        bucket(r, work)
        return carry

    lax.fori_loop(0, requests, one, 0)
    for h in range(heads_ref.shape[0]):
        block = ctx32[h].astype(BF16)
        heads_ref[h] = block
        flat_ref[:, h * 128 : (h + 1) * 128] = block


def attend(queries, cache_pages, window_kv, lengths, page_rows):
    requests, window, head_count, head_size = queries.shape
    q = queries.transpose(0, 2, 1, 3).reshape(requests, 2, head_count // 2 * window, head_size)
    rows = requests * window
    return pl.pallas_call(
        attend_kernel,
        out_shape=(
            jax.ShapeDtypeStruct((head_count, rows, head_size), BF16),
            jax.ShapeDtypeStruct((rows, head_count * head_size), BF16),
        ),
        in_specs=[sspec(), sspec(), vspec(), vspec(), aspec()],
        out_specs=(vspec(), vspec()),
        scratch_shapes=[
            pltpu.VMEM((requests, 16) + cache_pages.shape[1:], BF16),
            pltpu.VMEM((head_count, rows, head_size), F32),
            pltpu.SemaphoreType.DMA((requests,)),
        ],
        compiler_params=pltpu.CompilerParams(vmem_limit_bytes=40 * 2**20),
        cost_estimate=pl.CostEstimate(
            flops=12 * 10**9, bytes_accessed=10 * 2**20, transcendentals=10**6
        ),
        name="attend",
    )(lengths, page_rows, q, window_kv, cache_pages)


def own_block(shape):
    row = lax.broadcasted_iota(jnp.int32, shape, 0) // 8
    col = lax.broadcasted_iota(jnp.int32, shape, 1) // 64
    return row == col


def down_kernel(slot_ref, ctx_ref, down_ref, z_ref):
    low = lax.broadcasted_iota(jnp.int32, (32, 128), 1) < 64
    keep = own_block((32, 256))

    def block(p, carry):
        parts = []
        for g in range(4):
            first = p * 16 + g * 4
            pages = jnp.concatenate([down_ref[slot_ref[first + a]] for a in range(4)], axis=0)
            rows = ctx_ref[p, g * 32 : (g + 1) * 32, :]
            wide = lax.dot_general(rows, pages, NT, preferred_element_type=F32)
            wide = jnp.where(keep, wide, 0.0)
            half = wide[:, 0:128] + wide[:, 128:256]
            parts.append(half + pltpu.roll(half, 64, 1))
        z_ref[p, 0:32, :] = jnp.where(low, parts[0], parts[2])
        z_ref[p, 32:64, :] = jnp.where(low, parts[1], parts[3])
        return carry

    lax.fori_loop(0, ctx_ref.shape[0], block, 0)


def up_kernel(slot_ref, z_ref, up_ref, out_ref):
    low = lax.broadcasted_iota(jnp.int32, (32, 128), 1) < 64
    keep = own_block((32, 256))

    def block(p, carry):
        parts = [None] * 4
        for half in range(2):
            x = z_ref[p, half * 32 : half * 32 + 32, :]
            turned = pltpu.roll(x, 64, 1)
            parts[half] = jnp.where(low, x, turned)
            parts[half + 2] = jnp.where(low, turned, x)
        for g in range(4):
            first = p * 16 + g * 4
            pages = jnp.concatenate([up_ref[slot_ref[first + a]] for a in range(4)], axis=0)
            twice = jnp.concatenate([parts[g], parts[g]], axis=1)
            rows = jnp.where(keep, twice, 0.0).astype(BF16)
            out = jnp.dot(rows, pages, preferred_element_type=F32)
            out_ref[p, g * 32 : (g + 1) * 32, :] = out.astype(BF16)
        return carry

    lax.fori_loop(0, z_ref.shape[0], block, 0)


def down_call(slots, ctx_all, down_all):
    n = ctx_all.shape[0]
    return pl.pallas_call(
        down_kernel,
        out_shape=jax.ShapeDtypeStruct((n, 64, 128), F32),
        in_specs=[sspec(), vspec(), vspec()],
        out_specs=vspec(),
        compiler_params=pltpu.CompilerParams(vmem_limit_bytes=16 * 2**20),
        cost_estimate=pl.CostEstimate(
            flops=4 * 10**9, bytes_accessed=3 * 2**20, transcendentals=0
        ),
        name="rank_down",
    )(slots, ctx_all, down_all)


def up_call(slots, z, up_all):
    n = z.shape[0]
    return pl.pallas_call(
        up_kernel,
        out_shape=jax.ShapeDtypeStruct((n, 128, 128), BF16),
        in_specs=[sspec(), vspec(), vspec()],
        out_specs=vspec(),
        compiler_params=pltpu.CompilerParams(vmem_limit_bytes=16 * 2**20),
        cost_estimate=pl.CostEstimate(
            flops=4 * 10**9, bytes_accessed=3 * 2**20, transcendentals=0
        ),
        name="rank_up",
    )(slots, z, up_all)


def spread_columns(pages):
    count, rank, width = pages.shape
    n = lax.axis_size("pool")
    x = pages.reshape(count * rank, n, width // n).transpose(1, 0, 2)
    x = lax.all_to_all(x, "pool", split_axis=0, concat_axis=0, tiled=True)
    return x.reshape(n * count, rank, width // n)


def per_device(
    hidden,
    queries,
    window_key_value,
    cached_key_value,
    cached_length,
    request_page_table,
    request_adapter,
    layer_page_slot,
    wo,
    adapter_down,
    adapter_up,
):
    section_count = lax.axis_size("section")
    section_index = lax.axis_index("section")
    adapters = layer_page_slot.shape[0] // section_count
    layer_start = section_index * adapters
    down_all = spread_columns(adapter_down)
    up_all = spread_columns(adapter_up)
    slots = (
        layer_page_slot[layer_start + request_adapter[section_index].reshape(-1)] - layer_start
    ).astype(jnp.int32)
    heads, flat = attend(
        queries[0, 0],
        cached_key_value[0, 0],
        window_key_value[0, 0],
        cached_length[0, 0],
        request_page_table[0, 0],
    )
    ctx_all = lax.all_to_all(heads, "pool", split_axis=0, concat_axis=0, tiled=True)
    partial_out = jnp.dot(flat, wo[0], preferred_element_type=F32)
    plain_output = lax.psum_scatter(partial_out, "tp", scatter_dimension=1, tiled=True)
    z = down_call(slots, ctx_all, down_all)
    z = lax.psum(z, ("tp", "pool"))
    z = z.astype(BF16).astype(F32)
    delta = up_call(slots, z, up_all)
    back = lax.all_to_all(delta, "pool", split_axis=0, concat_axis=0, tiled=True)
    rows, width = hidden.shape[2:]
    adapter_delta = back.transpose(1, 0, 2).reshape(rows, width).astype(F32)
    blended = (hidden[0, 0].astype(F32) + plain_output + adapter_delta).astype(BF16)
    handed = lax.ppermute(
        blended, "section", [(k, (k + 1) % section_count) for k in range(section_count)]
    )
    return handed[None, None]


def solution(mesh):
    return jax.shard_map(
        per_device,
        mesh=mesh,
        in_specs=(
            P("section", "pool", None, "tp"),
            P("section", "pool", None, None, "tp", None),
            P("section", "pool", None, None, "tp", None, None),
            P("section", "pool", None, None, "tp", None, None),
            P("section", "pool", None),
            P("section", "pool", None, None),
            P(),
            P(),
            P("section", "tp", None),
            P(("section", "pool"), None, "tp"),
            P(("section", "pool"), None, "tp"),
        ),
        out_specs=P("section", "pool", None, "tp"),
        check_vma=False,
    )
```

time: 321 us -> 512 us (1.60)
  blocking collectives: 18.2 us -> 317 us
  waiting for transfers between devices: 168 us -> 32.3 us
  starting transfers between devices: 12.1 us -> 76 us
  Pallas kernels: 0 us -> 34.6 us
  matrix products: 48.3 us -> 17 us
  other arithmetic: 32.9 us -> 1.64 us
  local copies, waits for them, and re-layouts: 25 us -> 18.8 us
    psum x1, blocking collectives: 18.2 us -> 305 us  [per_device(): z = lax.psum(z, ('tp', 'pool'))]
    all_gather x1 -> x0, waiting for transfers between devices: 71.9 us -> none  [per_device(): everyone = lax.all_gather(context, 'pool', axis=0, tiled=True)]
    all_to_all x1 -> x3, waiting for transfers between devices: 94.3 us -> 30.8 us  [the longest x2 24.1 us: spread_columns(): x = lax.all_to_all(x, 'pool', split_axis=0, concat_axis=0, tiled=True)]
    ppermute x1, starting transfers between devices: 6.98 us -> 57.7 us  [per_device(): lax.ppermute(blended, 'section', [(k, (k + 1) % section_count) for k in r...]
    pallas_call x0 -> x3, Pallas kernels: none -> 34.6 us  [the longest x1 24.5 us: attend(): pl.pallas_call(attend_kernel, out_shape=(jax.ShapeDtypeStruct((head_count...]
    dot_general x4 -> x1, matrix products: 40.2 us -> 17 us  [per_device(): partial_out = jnp.dot(flat, wo[0], preferred_element_type=F32)]
    select_n x3 -> x1, other arithmetic: 15 us -> 0.01 us  [per_device(): layer_page_slot[layer_start + request_adapter[section_index].reshape(-1)]]
    all_to_all x1 -> x3, starting transfers between devices: 5.06 us -> 18.3 us  [the longest x2 9.53 us: spread_columns(): x = lax.all_to_all(x, 'pool', split_axis=0, concat_axis=0, tiled=True)]
  transfers between devices with their start and end apart: 4 -> 5, of which waited for: 3 -> 3; matrix products, arithmetic and copies ran while one was open for 8% -> 2% of each run, Pallas kernels for 0% -> 2%
where the time goes in v1:
time: 512 us; the launch traced here: 511 us
  blocking collectives  317 us (62%)
  starting transfers between devices  76 us (15%)
  Pallas kernels  34.6 us (7%)
  waiting for transfers between devices  32.3 us (6%)
  local copies, waits for them, and re-layouts  18.8 us (4%)
  matrix products  17 us (3%)
  between operations  13.6 us (3%)
    psum x1, blocking collectives, per_device(): z = lax.psum(z, ('tp', 'pool'))  305 us
    ppermute x1, starting transfers between devices, per_device(): lax.ppermute(blended, 'section', [(k, (k + 1) % section_count) for k in r...  57.7 us
    pallas_call x1, Pallas kernels, attend(): pl.pallas_call(attend_kernel, out_shape=(jax.ShapeDtypeStruct((head_count...  24.5 us
    all_to_all x2, waiting for transfers between devices, spread_columns(): x = lax.all_to_all(x, 'pool', split_axis=0, concat_axis=0, tiled=True)  24.1 us
    dot_general x1, matrix products, per_device(): partial_out = jnp.dot(flat, wo[0], preferred_element_type=F32)  17 us
    all_to_all x1, blocking collectives, per_device(): lax.all_to_all(delta, 'pool', split_axis=0, concat_axis=0, tiled=True)  11.7 us
    unnamed x17, local copies, waits for them, and re-layouts  11.2 us
  transfers between devices with their start and end apart: 5, of which 3 were waited for; matrix products, arithmetic and copies ran while one was open for 2% of the time, Pallas kernels for 2%

profile of v1, /device:TPU:1, one launch (start us, length us, event | category | flops | bytes accessed | tf_op | source)
XLA Modules:
  0.0 510.7 jit_solution(1434556586023728772)
XLA Ops:
  6.5 0.0 copy-start
  6.5 0.0 reduce-scatter.2.cloned.1.call-start
  6.5 1.2 copy.15
  7.7 0.0 copy-start.1
  7.7 3.4 copy-done.1
  11.1 0.0 copy-start.2
  11.1 0.9 copy-done.2
  12.0 0.0 copy-start.3
  12.0 0.7 copy-done.3
  12.7 0.0 copy-start.4
  12.7 0.7 copy-done.4
  13.4 24.5 %attend.1 = (bf16[16,128,128]{2,1,0:T(8,128)(2,1)}, bf16[128,2048]{1,0:T(8,128)(2,1)S(1)}) custom-call(s32[16]{0:T(128)S(1)} %bitcast.39, s32[16,16]{1,0:T(8,128)S(1)} %bitcast.38, bf16[16,2,64,128]{3,2,1,0:T(8,128)(2,1)S(1)} %bitcast.35, bf16[16,2,2,8,128]{4,3,2,1,0:T(8,128)(2,1)S(1)} %bitcast.37, bf16[128,2,2,64,128]{4,3,2,1,0:T(8,128)(2,1)S(1)} %bitcast.36), custom_call_target="tpu_custom_call" | custom-call | flops 12000000000 | bytes 10485760 | tf_op jit(solution)/shard_map/attend/pallas_call | solution.py:123
  37.9 17.0 %fusion = f32[128,8192]{1,0:T(8,128)} fusion(bf16[128,2048]{1,0:T(8,128)(2,1)S(1)} %get-tuple-element.7, bf16[1,2048,8192]{2,1,0:T(8,128)(2,1)} %param.19), kind=kOutput, calls=%fused_computation.1 | convolution fusion | flops 4294967296 | bytes 38273024 | tf_op jit(solution)/shard_map/dot_general | solution.py:262
  55.0 0.0 reduce-scatter.2.cloned.1.call-update
  55.0 8.7 %all-to-all-start = ((bf16[16,128,128]{2,1,0:T(8,128)(2,1)}), bf16[16,128,128]{2,1,0:T(8,128)(2,1)S(1)}, u32[]{:S(2)}, u32[]{:S(2)}) async-start(bf16[16,128,128]{2,1,0:T(8,128)(2,1)} %get-tuple-element.8), calls=%async_computation.1 | async-start | bytes 1048576 | tf_op jit(solution)/shard_map/all_to_all | solution.py:261
  63.7 2.2 copy.20
  66.0 1.9 copy.25
  67.8 6.6 %all-to-all-done.ctx_ref = bf16[16,128,128]{2,1,0:T(8,128)(2,1)S(1)} async-done(((bf16[16,128,128]{2,1,0:T(8,128)(2,1)}), bf16[16,128,128]{2,1,0:T(8,128)(2,1)S(1)}, u32[]{:S(2)}, u32[]{:S(2)}) %all-to-all-start) | async-done | bytes 524320 | tf_op jit(solution)/shard_map/all_to_all | solution.py:261
  74.5 3.7 all-to-all-start.1
  78.2 2.2 copy.21
  80.4 1.9 copy.24
  82.3 24.1 %all-to-all-done.1 = bf16[16,512,128]{2,1,0:T(8,128)(2,1)S(1)} async-done(((bf16[16,512,128]{2,1,0:T(8,128)(2,1)}), bf16[16,512,128]{2,1,0:T(8,128)(2,1)S(1)}, u32[]{:S(2)}, u32[]{:S(2)}) %all-to-all-start.1) | async-done | bytes 2097184 | tf_op jit(solution)/shard_map/all_to_all | solution.py:228
  106.4 0.0 copy-start.6
  106.4 5.8 %all-to-all-start.2 = ((bf16[16,512,128]{2,1,0:T(8,128)(2,1)}), bf16[16,512,128]{2,1,0:T(8,128)(2,1)}, u32[]{:S(2)}, u32[]{:S(2)}) async-start(bf16[16,512,128]{2,1,0:T(8,128)(2,1)} %bitcast.40), calls=%async_computation.3 | async-start | bytes 4194304 | tf_op jit(solution)/shard_map/all_to_all | solution.py:228
  112.2 0.0 copy-done.6
  112.3 0.1 add.48
  112.4 0.0 copy-done
  112.4 1.9 gather_fusion
  114.3 4.9 rank_down.1
  119.2 305.0 %all-reduce.1 = bf16[16,64,128]{2,1,0:T(8,128)(2,1)S(1)} all-reduce(f32[16,64,128]{2,1,0:T(8,128)S(1)} %rank_down.1), channel_id=1, replica_groups=mesh['section'=2,'tp'=4,'pool'=16] {'tp','pool'}, use_global_device_ids=true, to_apply=%region_1.0 | all-reduce | flops 131072 | bytes 786432 | tf_op jit(solution)/shard_map/psum | solution.py:265
  424.3 0.0 all-to-all-done.2
  424.3 5.2 %rank_up.1 = bf16[16,128,128]{2,1,0:T(8,128)(2,1)S(1)} custom-call(s32[256]{0:T(256)S(1)} %broadcast_subtract_fusion.slot_ref, f32[16,64,128]{2,1,0:T(8,128)S(1)} %convert_element_type.39.z_ref, bf16[128,64,128]{2,1,0:T(8,128)(2,1)} %bitcast.13.up_ref), custom_call_target="tpu_custom_call" | custom-call | flops 4000000000 | bytes 3145728 | tf_op jit(solution)/shard_map/rank_up/pallas_call | solution.py:211
  429.5 11.7 %all_to_all.20 = bf16[16,128,128]{2,1,0:T(8,128)(2,1)S(1)} all-to-all(bf16[16,128,128]{2,1,0:T(8,128)(2,1)S(1)} %rank_up.1), channel_id=1, replica_groups=mesh['section'=2,'tp'=4,'pool'=16] {'pool'}, dimensions={0} | all-to-all | bytes 1048576 | tf_op jit(solution)/shard_map/all_to_all | solution.py:268
  441.2 0.1 convert_bitcast_fusion
  441.3 0.0 copy-start.5
  441.3 0.3 copy.18
  441.7 0.3 copy.19
  442.0 0.0 reduce-scatter.2.cloned.1.call-done
  442.0 0.3 copy-done.5
  442.4 1.5 fusion.3
  443.8 57.7 %collective-permute-start = (bf16[128,2048]{1,0:T(8,128)(2,1)S(1)}, bf16[128,2048]{1,0:T(8,128)(2,1)S(1)}, u32[]{:S(2)}, u32[]{:S(2)}) collective-permute-start(bf16[128,2048]{1,0:T(8,128)(2,1)S(1)} %fusion.3), channel_id=1, source_target_pairs={{0,64},{64,0},{1,65},{65,1},{2,66},{66,2},{3,67},{67,3},{4,68},{68... | collective-permute-start | bytes 1572872 | tf_op jit(solution)/shard_map/ppermute | solution.py:272
  501.6 1.5 collective-permute-done
  503.1 0.8 copy.29
  (5 shorter events, 0.1 us)
Async XLA Ops:
  6.5 105.8 %copy-start = (s32[256]{0:T(256)S(1)}, s32[256]{0:T(256)}, u32[]{:S(2)}) copy-start(s32[256]{0:T(256)} %param.18) | copy-start | bytes 3076
  6.5 435.5 %reduce-scatter.2.cloned.1.call-start = ((), (), s32[]{:S(2)}) async-start(), calls=%async_computation.5 | async-start | bytes 5242880 | tf_op jit(solution)/shard_map/reduce_scatter | solution.py:263
  7.7 3.4 copy-start.1
  11.1 0.9 copy-start.2
  12.0 0.7 copy-start.3
  12.7 0.7 copy-start.4
  55.0 19.5 %all-to-all-start = ((bf16[16,128,128]{2,1,0:T(8,128)(2,1)}), bf16[16,128,128]{2,1,0:T(8,128)(2,1)S(1)}, u32[]{:S(2)}, u32[]{:S(2)}) async-start(bf16[16,128,128]{2,1,0:T(8,128)(2,1)} %get-tuple-element.8), calls=%async_computation.1 | async-start | bytes 1048576 | tf_op jit(solution)/shard_map/all_to_all | solution.py:261
  74.5 31.9 %all-to-all-start.1 = ((bf16[16,512,128]{2,1,0:T(8,128)(2,1)}), bf16[16,512,128]{2,1,0:T(8,128)(2,1)S(1)}, u32[]{:S(2)}, u32[]{:S(2)}) async-start(bf16[16,512,128]{2,1,0:T(8,128)(2,1)} %bitcast.41), calls=%async_computation.2 | async-start | bytes 4194304 | tf_op jit(solution)/shard_map/all_to_all | solution.py:228
  106.4 5.8 %copy-start.6 = (s32[2,16,16]{2,1,0:T(8,128)S(1)}, s32[2,16,16]{2,1,0:T(8,128)}, u32[]{:S(2)}) copy-start(s32[2,16,16]{2,1,0:T(8,128)} %param.17) | copy-start | bytes 6148
  106.4 317.9 %all-to-all-start.2 = ((bf16[16,512,128]{2,1,0:T(8,128)(2,1)}), bf16[16,512,128]{2,1,0:T(8,128)(2,1)}, u32[]{:S(2)}, u32[]{:S(2)}) async-start(bf16[16,512,128]{2,1,0:T(8,128)(2,1)} %bitcast.40), calls=%async_computation.3 | async-start | bytes 4194304 | tf_op jit(solution)/shard_map/all_to_all | solution.py:228
  441.3 1.0 copy-start.5
  443.8 59.3 %collective-permute-start = (bf16[128,2048]{1,0:T(8,128)(2,1)S(1)}, bf16[128,2048]{1,0:T(8,128)(2,1)S(1)}, u32[]{:S(2)}, u32[]{:S(2)}) collective-permute-start(bf16[128,2048]{1,0:T(8,128)(2,1)S(1)} %fusion.3), channel_id=1, source_target_pairs={{0,64},{64,0},{1,65},{65,1},{2,66},{66,2},{3,67},{67,3},{4,68},{68... | collective-permute-start | bytes 1572872 | tf_op jit(solution)/shard_map/ppermute | solution.py:272
Sparse Core Ops, SparseCore 0:
  55.1 49.7 reduce-scatter.1

commit v2 on v0

v2 whole, which is shorter than its diff:
```python
import functools

import jax
import jax.numpy as jnp
from jax import lax
from jax.experimental import pallas as pl
from jax.experimental.pallas import tpu as pltpu
from jax.sharding import PartitionSpec as P

F32 = jnp.float32
BF16 = jnp.bfloat16
NT = (((1,), (1,)), ((), ()))
TN = (((0,), (0,)), ((), ()))
MESH = pl.DeviceIdType.MESH
SIDE = 4
POOL = SIDE * SIDE
SELF = 10
HEAD = 128
TILE = 512
BUFS = 3
BATCH = ((0, 4), (4, 9), (9, 16))


def own_block(shape):
    row = lax.broadcasted_iota(jnp.int32, shape, 0) // 8
    col = lax.broadcasted_iota(jnp.int32, shape, 1) // 64
    return row == col


def attend_one(r, len_ref, table_ref, q_ref, wkv_ref, cache_ref, ctx32):
    scale = HEAD ** (-0.5)
    pages = table_ref.shape[3]
    length = len_ref[0, 0, r]
    zero = jnp.zeros(q_ref.shape[2:], BF16)
    query = jnp.concatenate(
        [
            jnp.concatenate([q_ref[r, 0], zero], axis=1),
            jnp.concatenate([zero, q_ref[r, 1]], axis=1),
        ],
        axis=0,
    )
    window_key = jnp.concatenate([wkv_ref[r, 0, 0], wkv_ref[r, 0, 1]], axis=1)
    window_value = jnp.concatenate([wkv_ref[r, 1, 0], wkv_ref[r, 1, 1]], axis=1)

    def side(kv):
        return jnp.concatenate(
            [
                jnp.concatenate(
                    [
                        cache_ref[table_ref[0, 0, r, j], kv, 0],
                        cache_ref[table_ref[0, 0, r, j], kv, 1],
                    ],
                    axis=1,
                )
                for j in range(pages)
            ],
            axis=0,
        )

    s = lax.dot_general(side(0), query, NT, preferred_element_type=F32) * scale
    position = lax.broadcasted_iota(jnp.int32, s.shape, 0)
    s = jnp.where(position < length, s, -1e30)
    sw = lax.dot_general(window_key, query, NT, preferred_element_type=F32) * scale
    row = lax.broadcasted_iota(jnp.int32, sw.shape, 0)
    token = lax.broadcasted_iota(jnp.int32, sw.shape, 1) % 8
    sw = jnp.where(row <= token, sw, -1e30)
    top = jnp.maximum(jnp.max(s, axis=0, keepdims=True), jnp.max(sw, axis=0, keepdims=True))
    p = jnp.exp(s - top)
    pw = jnp.exp(sw - top)
    total = jnp.sum(p, axis=0, keepdims=True) + jnp.sum(pw, axis=0, keepdims=True)
    inverse = 1.0 / total
    p = (p * inverse).astype(BF16)
    pw = (pw * inverse).astype(BF16)
    out = lax.dot_general(p, side(1), TN, preferred_element_type=F32)
    out = out + lax.dot_general(pw, window_value, TN, preferred_element_type=F32)
    rows = pl.ds(pl.multiple_of(r * 8, 8), 8)
    ctx32[0:8, rows, :] = out[0:64, 0:128].reshape(8, 8, 128)
    ctx32[8:16, rows, :] = out[64:128, 128:256].reshape(8, 8, 128)


def kernel(
    len_ref,
    table_ref,
    adapter_ref,
    layer_ref,
    q_ref,
    wkv_hbm,
    cache_hbm,
    down_hbm,
    up_hbm,
    hidden_hbm,
    wo_hbm,
    out_ref,
    cache,
    wkv,
    hidden,
    down_stage,
    up_stage,
    down_all,
    up_all,
    ctx32,
    heads,
    flat,
    ctx_all,
    wbuf,
    far_send,
    far_recv,
    part,
    near_send,
    near_recv,
    own,
    z_send,
    z_recv,
    zt_send,
    zt_recv,
    z_own,
    z_all,
    delta_send,
    delta_recv,
    final,
    lsem,
    wsem,
    down_s,
    down_r,
    up_s,
    up_r,
    ctx_s,
    ctx_r,
    z_s,
    z_r,
    za_s,
    za_r,
    delta_s,
    delta_r,
    tp_s,
    tp_r,
    zt_s,
    zt_r,
    sec_s,
    sec_r,
):
    me = lax.axis_index("pool")
    x = lax.axis_index("tp")
    sec = lax.axis_index("section")
    mz = me // SIDE
    my = lax.rem(me, SIDE)
    adapters = layer_ref.shape[0] // 2
    start = sec * adapters

    def slot(p, r):
        return lax.rem(layer_ref[start + adapter_ref[sec, p, r]], adapters)

    def peer(k):
        dz = k // SIDE + 2
        dy = lax.rem(k, SIDE) + 2
        return lax.rem(mz + dz, SIDE) * SIDE + lax.rem(my + dy, SIDE)

    def origin(k):
        dz = 6 - k // SIDE
        dy = 6 - lax.rem(k, SIDE)
        return lax.rem(mz + dz, SIDE) * SIDE + lax.rem(my + dy, SIDE)

    def each(low, high, fn):
        def step(k, carry):
            fn(k)
            return carry

        if low < SELF < high:
            lax.fori_loop(low, SELF, step, 0)
            lax.fori_loop(SELF + 1, high, step, 0)
        else:
            lax.fori_loop(low + (low == SELF), high - (high == SELF + 1), step, 0)

    def pool_copy(src, dst, ssem, rsem, k, to):
        return pltpu.make_async_remote_copy(
            src_ref=src,
            dst_ref=dst,
            send_sem=ssem.at[k],
            recv_sem=rsem.at[k],
            device_id={"pool": to},
            device_id_type=MESH,
        )

    def columns(ref, j):
        return ref.at[:, :, pl.ds(pl.multiple_of(j * HEAD, HEAD), HEAD)]

    held = down_hbm.shape[0]

    def pages_of(ref, j):
        return ref.at[pl.ds(j * held, held)]

    def stage_copy(ref, stage, full, k, base):
        j = peer(k)
        return pltpu.make_async_copy(columns(ref, j), stage.at[j], lsem.at[base + k])

    def own_copy(ref, full, base):
        return pltpu.make_async_copy(columns(ref, me), pages_of(full, me), lsem.at[base + SELF])

    quarter = cache.shape[0] // 4

    def cache_copy(i):
        return pltpu.make_async_copy(
            cache_hbm.at[0, 0, i * quarter : (i + 1) * quarter],
            cache.at[i * quarter : (i + 1) * quarter],
            lsem.at[32 + i],
        )

    wkv_copy = pltpu.make_async_copy(wkv_hbm.at[0, 0], wkv, lsem.at[36])
    hidden_copy = pltpu.make_async_copy(hidden_hbm.at[0, 0], hidden, lsem.at[37])

    each(0, POOL, lambda k: stage_copy(down_hbm, down_stage, down_all, k, 0).start())
    own_copy(down_hbm, down_all, 0).start()
    wkv_copy.start()
    for i in range(4):
        cache_copy(i).start()

    barrier = pltpu.get_barrier_semaphore()

    def greet(k):
        pl.semaphore_signal(barrier, inc=1, device_id={"pool": peer(k)}, device_id_type=MESH)

    each(0, POOL, greet)
    for o in (1, 2, 3):
        pl.semaphore_signal(
            barrier, inc=1, device_id={"tp": lax.rem(x + o, SIDE)}, device_id_type=MESH
        )
    pl.semaphore_signal(barrier, inc=1, device_id={"section": 1 - sec}, device_id_type=MESH)
    pl.semaphore_wait(barrier, POOL - 1 + 3 + 1)

    def send_down(k):
        stage_copy(down_hbm, down_stage, down_all, k, 0).wait()
        pool_copy(down_stage.at[peer(k)], pages_of(down_all, me), down_s, down_r, k, peer(k)).start()

    each(0, POOL, send_down)
    own_copy(down_hbm, down_all, 0).wait()

    wkv_copy.wait()
    for i in range(4):
        cache_copy(i).wait()

    each(0, POOL, lambda k: stage_copy(up_hbm, up_stage, up_all, k, 16).start())
    own_copy(up_hbm, up_all, 16).start()
    hidden_copy.start()

    def wo_copy(i):
        target = lax.rem(x + (2, 1, 3, 0)[i // 4], SIDE)
        col = target * (SIDE * TILE) + (i % 4) * TILE
        return pltpu.make_async_copy(
            wo_hbm.at[0, :, pl.ds(pl.multiple_of(col, TILE), TILE)],
            wbuf.at[i % BUFS],
            wsem.at[i % BUFS],
        )

    for i in range(BUFS):
        wo_copy(i).start()

    def attend_step(r, carry):
        attend_one(r, len_ref, table_ref, q_ref, wkv, cache, ctx32)
        return carry

    lax.fori_loop(0, q_ref.shape[0], attend_step, 0)
    for h in range(POOL):
        block = ctx32[h].astype(BF16)
        heads[h] = block
        flat[:, h * HEAD : (h + 1) * HEAD] = block

    def send_ctx(k):
        pool_copy(heads.at[peer(k)], ctx_all.at[me], ctx_s, ctx_r, k, peer(k)).start()

    each(0, POOL, send_ctx)
    ctx_all[me] = heads[me]

    def send_up(k):
        stage_copy(up_hbm, up_stage, up_all, k, 16).wait()
        pool_copy(up_stage.at[peer(k)], pages_of(up_all, me), up_s, up_r, k, peer(k)).start()

    each(*BATCH[0], send_up)
    own_copy(up_hbm, up_all, 16).wait()

    def wo_tile(i):
        wo_copy(i).wait()
        value = jnp.dot(flat[...], wbuf[i % BUFS], preferred_element_type=F32)
        cols = slice((i % 4) * TILE, (i % 4 + 1) * TILE)
        group = i // 4
        if group == 0:
            far_send[:, cols] = value.astype(BF16)
        elif group == 3:
            own[:, cols] = value
        else:
            part[group - 1, :, cols] = value
        if i + BUFS < 16:
            wo_copy(i + BUFS).start()

    def tp_copy(src, dst, i, step):
        return pltpu.make_async_remote_copy(
            src_ref=src,
            dst_ref=dst,
            send_sem=tp_s.at[i],
            recv_sem=tp_r.at[i],
            device_id={"tp": lax.rem(x + SIDE + step, SIDE)},
            device_id_type=MESH,
        )

    def far_copy(i, step):
        return tp_copy(far_send.at[pl.ds(i * 64, 64)], far_recv.at[i], i, step)

    def near_copy(i, step):
        return tp_copy(near_send.at[i], near_recv.at[i], 2 + i, step)

    for i in range(4):
        wo_tile(i)
    far_copy(0, 1).start()
    far_copy(1, -1).start()
    for i in range(4, 12):
        wo_tile(i)
    far_copy(0, 1).wait_recv()
    far_copy(1, -1).wait_recv()
    near_send[0, 0:64] = (part[0, 0:64] + far_recv[0].astype(F32)).astype(BF16)
    near_send[0, 64:128] = part[0, 64:128].astype(BF16)
    near_send[1, 0:64] = part[1, 0:64].astype(BF16)
    near_send[1, 64:128] = (part[1, 64:128] + far_recv[1].astype(F32)).astype(BF16)
    near_copy(0, 1).start()
    near_copy(1, -1).start()

    def wait_ctx(k):
        s = origin(k)
        pool_copy(heads.at[s], ctx_all.at[s], ctx_s, ctx_r, k, s).wait_recv()

    def wait_down(k):
        s = origin(k)
        pool_copy(down_stage.at[s], pages_of(down_all, s), down_s, down_r, k, s).wait_recv()

    each(0, POOL, wait_down)
    each(0, POOL, wait_ctx)

    low = lax.broadcasted_iota(jnp.int32, (32, 128), 1) < 64
    keep = own_block((32, 256))

    def gathered(ref, p, g):
        return jnp.concatenate([ref[slot(p, g * 4 + a)] for a in range(4)], axis=0)

    def down_block(p, carry):
        pieces = []
        for g in range(4):
            pages = gathered(down_all, p, g)
            rows = ctx_all[p, g * 32 : (g + 1) * 32, :]
            wide = lax.dot_general(rows, pages, NT, preferred_element_type=F32)
            wide = jnp.where(keep, wide, 0.0)
            half = wide[:, 0:128] + wide[:, 128:256]
            pieces.append(half + pltpu.roll(half, 64, 1))
        z_send[p, 0:32, :] = jnp.where(low, pieces[0], pieces[2]).astype(BF16)
        z_send[p, 32:64, :] = jnp.where(low, pieces[1], pieces[3]).astype(BF16)
        return carry

    lax.fori_loop(0, POOL, down_block, 0)

    def send_z(k):
        pool_copy(z_send.at[peer(k)], z_recv.at[me], z_s, z_r, k, peer(k)).start()

    each(0, POOL, send_z)
    z_recv[me] = z_send[me]
    each(*BATCH[1], send_up)

    for i in range(12, 14):
        wo_tile(i)

    def wait_z(k):
        s = origin(k)
        pool_copy(z_send.at[s], z_recv.at[s], z_s, z_r, k, s).wait_recv()

    each(0, POOL, wait_z)
    total = z_recv[0].astype(F32)
    for p in range(1, POOL):
        total = total + z_recv[p].astype(F32)
    zt_send[...] = total.astype(BF16)

    def zt_copy(o):
        return pltpu.make_async_remote_copy(
            src_ref=zt_send,
            dst_ref=zt_recv.at[o - 1],
            send_sem=zt_s.at[o - 1],
            recv_sem=zt_r.at[o - 1],
            device_id={"tp": lax.rem(x + o, SIDE)},
            device_id_type=MESH,
        )

    for o in (2, 1, 3):
        zt_copy(o).start()
    for i in range(14, 16):
        wo_tile(i)
    for o in (1, 2, 3):
        zt_copy(o).wait_recv()
    total = zt_send[...].astype(F32)
    for o in range(3):
        total = total + zt_recv[o].astype(F32)
    z_own[...] = total.astype(BF16)

    def send_za(k):
        pool_copy(z_own, z_all.at[me], za_s, za_r, k, peer(k)).start()

    each(0, POOL, send_za)
    z_all[me] = z_own[...]
    each(*BATCH[2], send_up)

    hidden_copy.wait()
    near_copy(0, 1).wait_recv()
    near_copy(1, -1).wait_recv()
    own[...] = (
        own[...]
        + hidden[...].astype(F32)
        + near_recv[0].astype(F32)
        + near_recv[1].astype(F32)
    )

    def wait_za(k):
        pool_copy(z_own, z_all.at[origin(k)], za_s, za_r, k, origin(k)).wait_recv()

    def wait_up(k):
        s = origin(k)
        pool_copy(up_stage.at[s], pages_of(up_all, s), up_s, up_r, k, s).wait_recv()

    each(0, POOL, wait_za)
    each(0, POOL, wait_up)

    def up_block(p):
        pieces = [None] * 4
        for h in range(2):
            v = z_all[p, h * 32 : h * 32 + 32, :].astype(F32)
            turned = pltpu.roll(v, 64, 1)
            pieces[h] = jnp.where(low, v, turned)
            pieces[h + 2] = jnp.where(low, turned, v)
        for g in range(4):
            pages = gathered(up_all, p, g)
            twice = jnp.concatenate([pieces[g], pieces[g]], axis=1)
            rows = jnp.where(keep, twice, 0.0).astype(BF16)
            out = jnp.dot(rows, pages, preferred_element_type=F32)
            delta_send[p, g * 32 : (g + 1) * 32, :] = out.astype(BF16)

    def delta_copy(k, s, j):
        return pool_copy(delta_send.at[j], delta_recv.at[s], delta_s, delta_r, k, j)

    def up_and_send(k):
        up_block(peer(k))
        delta_copy(k, me, peer(k)).start()

    each(0, POOL, up_and_send)
    up_block(me)
    delta_recv[me] = delta_send[me]

    def wait_delta(k):
        s = origin(k)
        delta_copy(k, s, s).wait_recv()

    each(0, POOL, wait_delta)

    def hand_copy(h):
        rows = pl.ds(h * 64, 64)
        return pltpu.make_async_remote_copy(
            src_ref=final.at[rows],
            dst_ref=out_ref.at[rows],
            send_sem=sec_s.at[h],
            recv_sem=sec_r.at[h],
            device_id={"section": 1 - sec},
            device_id_type=MESH,
        )

    for h in range(2):
        rows = slice(h * 64, (h + 1) * 64)
        for j in range(POOL):
            cols = slice(j * HEAD, (j + 1) * HEAD)
            final[rows, cols] = (own[rows, cols] + delta_recv[j, rows].astype(F32)).astype(BF16)
        hand_copy(h).start()

    def drain(k):
        j = peer(k)
        pool_copy(down_stage.at[j], pages_of(down_all, me), down_s, down_r, k, j).wait_send()
        pool_copy(up_stage.at[j], pages_of(up_all, me), up_s, up_r, k, j).wait_send()
        pool_copy(heads.at[j], ctx_all.at[me], ctx_s, ctx_r, k, j).wait_send()
        pool_copy(z_send.at[j], z_recv.at[me], z_s, z_r, k, j).wait_send()
        pool_copy(z_own, z_all.at[me], za_s, za_r, k, j).wait_send()
        delta_copy(k, me, j).wait_send()

    each(0, POOL, drain)
    for o in (1, 2, 3):
        zt_copy(o).wait_send()
    far_copy(0, 1).wait_send()
    far_copy(1, -1).wait_send()
    near_copy(0, 1).wait_send()
    near_copy(1, -1).wait_send()
    for h in range(2):
        hand_copy(h).wait_send()
        hand_copy(h).wait_recv()


def per_device(
    hidden,
    queries,
    window_key_value,
    cached_key_value,
    cached_length,
    request_page_table,
    request_adapter,
    layer_page_slot,
    wo,
    adapter_down,
    adapter_up,
):
    requests, window, head_count, head_size = queries.shape[2:]
    rows = requests * window
    width = hidden.shape[3]
    q = queries[0, 0].transpose(0, 2, 1, 3)
    q = q.reshape(requests, 2, head_count // 2 * window, head_size)
    pages = adapter_down.shape[:2] + (HEAD,)
    smem = pl.BlockSpec(memory_space=pltpu.SMEM)
    vmem = pl.BlockSpec(memory_space=pltpu.VMEM)
    hbm = pl.BlockSpec(memory_space=pl.ANY)
    dma = pltpu.SemaphoreType.DMA
    handed = pl.pallas_call(
        kernel,
        out_shape=jax.ShapeDtypeStruct((rows, width), BF16),
        in_specs=[smem, smem, smem, smem, vmem, hbm, hbm, hbm, hbm, hbm, hbm],
        out_specs=vmem,
        scratch_shapes=[
            pltpu.VMEM(cached_key_value.shape[2:], BF16),
            pltpu.VMEM(window_key_value.shape[2:], BF16),
            pltpu.VMEM((rows, width), BF16),
            pltpu.VMEM((POOL,) + pages, BF16),
            pltpu.VMEM((POOL,) + pages, BF16),
            pltpu.VMEM((POOL * pages[0],) + pages[1:], BF16),
            pltpu.VMEM((POOL * pages[0],) + pages[1:], BF16),
            pltpu.VMEM((POOL, rows, HEAD), F32),
            pltpu.VMEM((POOL, rows, HEAD), BF16),
            pltpu.VMEM((rows, width), BF16),
            pltpu.VMEM((POOL, rows, HEAD), BF16),
            pltpu.VMEM((BUFS, width, TILE), BF16),
            pltpu.VMEM((rows, width), BF16),
            pltpu.VMEM((2, 64, width), BF16),
            pltpu.VMEM((2, rows, width), F32),
            pltpu.VMEM((2, rows, width), BF16),
            pltpu.VMEM((2, rows, width), BF16),
            pltpu.VMEM((rows, width), F32),
            pltpu.VMEM((POOL, 64, HEAD), BF16),
            pltpu.VMEM((POOL, 64, HEAD), BF16),
            pltpu.VMEM((64, HEAD), BF16),
            pltpu.VMEM((3, 64, HEAD), BF16),
            pltpu.VMEM((64, HEAD), BF16),
            pltpu.VMEM((POOL, 64, HEAD), BF16),
            pltpu.VMEM((POOL, rows, HEAD), BF16),
            pltpu.VMEM((POOL, rows, HEAD), BF16),
            pltpu.VMEM((rows, width), BF16),
            dma((40,)),
            dma((BUFS,)),
            dma((POOL,)),
            dma((POOL,)),
            dma((POOL,)),
            dma((POOL,)),
            dma((POOL,)),
            dma((POOL,)),
            dma((POOL,)),
            dma((POOL,)),
            dma((POOL,)),
            dma((POOL,)),
            dma((POOL,)),
            dma((POOL,)),
            dma((4,)),
            dma((4,)),
            dma((3,)),
            dma((3,)),
            dma((2,)),
            dma((2,)),
        ],
        compiler_params=pltpu.CompilerParams(
            collective_id=0, has_side_effects=True, vmem_limit_bytes=60 * 2**20
        ),
        name="relay_layer",
    )(
        cached_length,
        request_page_table,
        request_adapter,
        layer_page_slot,
        q,
        window_key_value,
        cached_key_value,
        adapter_down,
        adapter_up,
        hidden,
        wo,
    )
    return handed[None, None]


def solution(mesh):
    return jax.shard_map(
        per_device,
        mesh=mesh,
        in_specs=(
            P("section", "pool", None, "tp"),
            P("section", "pool", None, None, "tp", None),
            P("section", "pool", None, None, "tp", None, None),
            P("section", "pool", None, None, "tp", None, None),
            P("section", "pool", None),
            P("section", "pool", None, None),
            P(),
            P(),
            P("section", "tp", None),
            P(("section", "pool"), None, "tp"),
            P(("section", "pool"), None, "tp"),
        ),
        out_specs=P("section", "pool", None, "tp"),
        check_vma=False,
    )
```

time: 321 us -> 101 us (0.31)
  waiting for transfers between devices: 168 us -> 0 us
  Pallas kernels: 0 us -> 97.2 us
  matrix products: 48.3 us -> 0 us
  other arithmetic: 32.9 us -> 0 us
  local copies, waits for them, and re-layouts: 25 us -> 3.85 us
  blocking collectives: 18.2 us -> 0 us
  between operations: 15 us -> 0.01 us
  starting transfers between devices: 12.1 us -> 0 us
    pallas_call x0 -> x1, Pallas kernels: none -> 97.2 us  [per_device(): pl.pallas_call(kernel, out_shape=jax.ShapeDtypeStruct((rows, width), BF16...]
    all_to_all x1 -> x0, waiting for transfers between devices: 94.3 us -> none  [per_device(): lax.all_to_all(product.astype(jnp.bfloat16), 'pool', split_axis=0, concat...]
    all_gather x1 -> x0, waiting for transfers between devices: 71.9 us -> none  [per_device(): everyone = lax.all_gather(context, 'pool', axis=0, tiled=True)]
    dot_general x4 -> x0, matrix products: 40.2 us -> none  [the longest x1 17 us: per_device(): partial_out = jnp.dot(flat_rows, wo[0], preferred_element_type=jnp.float32)]
    psum x1 -> x0, blocking collectives: 18.2 us -> none  [per_device(): rank_hidden = lax.psum(rank_hidden, 'tp')]
    gather x2 -> x0, local copies, waits for them, and re-layouts: 15.1 us -> none  [the longest x1 13.1 us: attend(): picked = jnp.take(cache_pages, page_rows, axis=0)]
    select_n x3 -> x0, other arithmetic: 15 us -> none  [the longest x2 15 us: attend(): picked = jnp.take(cache_pages, page_rows, axis=0)]
    convert_element_type x3 -> x0, other arithmetic: 8.68 us -> none  [the longest x1 7.14 us: attend(): (weights / jnp.sum(weights, axis=-1, keepdims=True)).astype(jnp.bfloat16)]
  transfers between devices with their start and end apart: 4 -> 0, of which waited for: 3 -> 0; matrix products, arithmetic and copies ran while one was open for 8% -> 0% of each run, Pallas kernels for 0% -> 0%
where the time goes in v2:
time: 101 us
  Pallas kernels  97.2 us (96%)
  local copies, waits for them, and re-layouts  3.85 us (4%)
    pallas_call x1, Pallas kernels, per_device(): pl.pallas_call(kernel, out_shape=jax.ShapeDtypeStruct((rows, width), BF16...  97.2 us

profile of v2, /device:TPU:1, one launch (start us, length us, event | category | flops | bytes accessed | tf_op | source)
XLA Modules:
  0.0 101.1 jit_solution(13571317168682427606)
XLA Ops:
  0.0 2.0 %copy.12 = bf16[16,16,8,128]{3,2,1,0:T(8,128)(2,1)} copy(bf16[16,16,8,128]{3,1,2,0:T(8,128)(2,1)} %bitcast.7) | data formatting | bytes 1048576 | tf_op jit(solution)/shard_map/transpose | solution.py:511
  2.0 97.2 %relay_layer.1 = bf16[128,2048]{1,0:T(8,128)(2,1)} custom-call(s32[1,1,16]{2,1,0:T(1,128)} %len_ref.1, s32[1,1,16,16]{3,2,1,0:T(8,128)} %table_ref.1, s32[2,16,16]{2,1,0:T(8,128)} %adapter_ref.1, s32[256]{0:T(256)} %layer_ref.1, bf16[16,2,64,128]{3,2,1,0:T(8,128)(2,1)} %bitcast.6, bf16[1,1,16,2,2,8,128]{6,5,4,3,2,1,0:T(8,128)(2,1)} %wkv_hbm.1, ...), custom_call_target="tpu_custom_call" | custom-call | tf_op jit(solution)/shard_map/relay_layer/pallas_call | solution.py:518
  99.2 1.9 %copy.14 = bf16[1,1,128,2048]{3,2,1,0:T(8,128)(2,1)} copy(bf16[1,1,128,2048]{3,2,1,0:T(8,128)(2,1)} %bitcast.5) | data formatting | bytes 1048576

commit v3 on v2

--- a/solution.py
+++ b/solution.py
@@ -14,11 +14,16 @@
 MESH = pl.DeviceIdType.MESH
 SIDE = 4
 POOL = SIDE * SIDE
-SELF = 10
 HEAD = 128
 TILE = 512
 BUFS = 3
-BATCH = ((0, 4), (4, 9), (9, 16))
+OFFSETS = (
+    (2, 2), (1, 1), (3, 3), (1, 3), (3, 1),
+    (2, 1), (2, 3), (0, 2), (1, 0), (3, 0),
+    (1, 2), (3, 2), (2, 0), (0, 1), (0, 3),
+)
+EVEN = tuple(dz + SIDE * ((dy - dz) % SIDE) for dz, dy in OFFSETS)
+BATCH = (EVEN[:7], EVEN[7:11], EVEN[11:])
 
 
 def own_block(shape):
@@ -27,15 +32,16 @@
     return row == col
 
 
-def attend_one(r, len_ref, table_ref, q_ref, wkv_ref, cache_ref, ctx32):
+def attend_one(r, swap, len_ref, table_ref, q_ref, wkv_ref, cache_ref, ctx32):
     scale = HEAD ** (-0.5)
     pages = table_ref.shape[3]
     length = len_ref[0, 0, r]
-    zero = jnp.zeros(q_ref.shape[2:], BF16)
+    by_head = jnp.dot(swap, q_ref[r].reshape(128, HEAD), preferred_element_type=F32).astype(BF16)
+    zero = jnp.zeros((64, HEAD), BF16)
     query = jnp.concatenate(
         [
-            jnp.concatenate([q_ref[r, 0], zero], axis=1),
-            jnp.concatenate([zero, q_ref[r, 1]], axis=1),
+            jnp.concatenate([by_head[0:64], zero], axis=1),
+            jnp.concatenate([zero, by_head[64:128]], axis=1),
         ],
         axis=0,
     )
@@ -83,7 +89,7 @@
     table_ref,
     adapter_ref,
     layer_ref,
-    q_ref,
+    q_hbm,
     wkv_hbm,
     cache_hbm,
     down_hbm,
@@ -92,6 +98,7 @@
     wo_hbm,
     out_ref,
     cache,
+    q_ref,
     wkv,
     hidden,
     down_stage,
@@ -110,10 +117,11 @@
     near_recv,
     own,
     z_send,
-    z_recv,
-    zt_send,
-    zt_recv,
+    zx_recv,
+    zq_send,
+    zq_recv,
     z_own,
+    zq_all,
     z_all,
     delta_send,
     delta_recv,
@@ -134,6 +142,8 @@
     delta_r,
     tp_s,
     tp_r,
+    zx_s,
+    zx_r,
     zt_s,
     zt_r,
     sec_s,
@@ -151,13 +161,13 @@
         return lax.rem(layer_ref[start + adapter_ref[sec, p, r]], adapters)
 
     def peer(k):
-        dz = k // SIDE + 2
-        dy = lax.rem(k, SIDE) + 2
+        dz = lax.rem(k, SIDE)
+        dy = dz + k // SIDE
         return lax.rem(mz + dz, SIDE) * SIDE + lax.rem(my + dy, SIDE)
 
     def origin(k):
-        dz = 6 - k // SIDE
-        dy = 6 - lax.rem(k, SIDE)
+        dz = SIDE - lax.rem(k, SIDE)
+        dy = dz + SIDE - k // SIDE
         return lax.rem(mz + dz, SIDE) * SIDE + lax.rem(my + dy, SIDE)
 
     def each(low, high, fn):
@@ -165,11 +175,7 @@
             fn(k)
             return carry
 
-        if low < SELF < high:
-            lax.fori_loop(low, SELF, step, 0)
-            lax.fori_loop(SELF + 1, high, step, 0)
-        else:
-            lax.fori_loop(low + (low == SELF), high - (high == SELF + 1), step, 0)
+        lax.fori_loop(low, high, step, 0)
 
     def pool_copy(src, dst, ssem, rsem, k, to):
         return pltpu.make_async_remote_copy(
@@ -194,7 +200,7 @@
         return pltpu.make_async_copy(columns(ref, j), stage.at[j], lsem.at[base + k])
 
     def own_copy(ref, full, base):
-        return pltpu.make_async_copy(columns(ref, me), pages_of(full, me), lsem.at[base + SELF])
+        return pltpu.make_async_copy(columns(ref, me), pages_of(full, me), lsem.at[base])
 
     quarter = cache.shape[0] // 4
 
@@ -206,39 +212,45 @@
         )
 
     wkv_copy = pltpu.make_async_copy(wkv_hbm.at[0, 0], wkv, lsem.at[36])
+    query_copy = pltpu.make_async_copy(q_hbm.at[0, 0], q_ref, lsem.at[38])
     hidden_copy = pltpu.make_async_copy(hidden_hbm.at[0, 0], hidden, lsem.at[37])
 
-    each(0, POOL, lambda k: stage_copy(down_hbm, down_stage, down_all, k, 0).start())
+    for k in EVEN:
+        stage_copy(down_hbm, down_stage, down_all, k, 0).start()
     own_copy(down_hbm, down_all, 0).start()
+    query_copy.start()
     wkv_copy.start()
-    for i in range(4):
-        cache_copy(i).start()
 
     barrier = pltpu.get_barrier_semaphore()
 
     def greet(k):
         pl.semaphore_signal(barrier, inc=1, device_id={"pool": peer(k)}, device_id_type=MESH)
 
-    each(0, POOL, greet)
+    each(1, POOL, greet)
     for o in (1, 2, 3):
         pl.semaphore_signal(
             barrier, inc=1, device_id={"tp": lax.rem(x + o, SIDE)}, device_id_type=MESH
         )
     pl.semaphore_signal(barrier, inc=1, device_id={"section": 1 - sec}, device_id_type=MESH)
     pl.semaphore_wait(barrier, POOL - 1 + 3 + 1)
+    for i in range(4):
+        cache_copy(i).start()
 
     def send_down(k):
         stage_copy(down_hbm, down_stage, down_all, k, 0).wait()
         pool_copy(down_stage.at[peer(k)], pages_of(down_all, me), down_s, down_r, k, peer(k)).start()
 
-    each(0, POOL, send_down)
+    for k in EVEN:
+        send_down(k)
     own_copy(down_hbm, down_all, 0).wait()
 
+    query_copy.wait()
     wkv_copy.wait()
     for i in range(4):
         cache_copy(i).wait()
 
-    each(0, POOL, lambda k: stage_copy(up_hbm, up_stage, up_all, k, 16).start())
+    for k in EVEN:
+        stage_copy(up_hbm, up_stage, up_all, k, 16).start()
     own_copy(up_hbm, up_all, 16).start()
     hidden_copy.start()
 
@@ -254,8 +266,12 @@
     for i in range(BUFS):
         wo_copy(i).start()
 
+    to = lax.broadcasted_iota(jnp.int32, (128, 128), 0)
+    source = lax.broadcasted_iota(jnp.int32, (128, 128), 1)
+    swap = jnp.where(source == (to % 8) * 16 + to // 8, 1.0, 0.0).astype(BF16)
+
     def attend_step(r, carry):
-        attend_one(r, len_ref, table_ref, q_ref, wkv, cache, ctx32)
+        attend_one(r, swap, len_ref, table_ref, q_ref, wkv, cache, ctx32)
         return carry
 
     lax.fori_loop(0, q_ref.shape[0], attend_step, 0)
@@ -267,14 +283,16 @@
     def send_ctx(k):
         pool_copy(heads.at[peer(k)], ctx_all.at[me], ctx_s, ctx_r, k, peer(k)).start()
 
-    each(0, POOL, send_ctx)
+    for k in EVEN:
+        send_ctx(k)
     ctx_all[me] = heads[me]
 
     def send_up(k):
         stage_copy(up_hbm, up_stage, up_all, k, 16).wait()
         pool_copy(up_stage.at[peer(k)], pages_of(up_all, me), up_s, up_r, k, peer(k)).start()
 
-    each(*BATCH[0], send_up)
+    for k in BATCH[0]:
+        send_up(k)
     own_copy(up_hbm, up_all, 16).wait()
 
     def wo_tile(i):
@@ -304,8 +322,10 @@
     def far_copy(i, step):
         return tp_copy(far_send.at[pl.ds(i * 64, 64)], far_recv.at[i], i, step)
 
-    def near_copy(i, step):
-        return tp_copy(near_send.at[i], near_recv.at[i], 2 + i, step)
+    def near_copy(i, half):
+        rows = pl.ds(half * 64, 64)
+        src, dst = near_send.at[i, rows], near_recv.at[i, rows]
+        return tp_copy(src, dst, 2 + 2 * i + half, 1 - 2 * i)
 
     for i in range(4):
         wo_tile(i)
@@ -313,14 +333,14 @@
     far_copy(1, -1).start()
     for i in range(4, 12):
         wo_tile(i)
+    near_send[0, 64:128] = part[0, 64:128].astype(BF16)
+    near_send[1, 0:64] = part[1, 0:64].astype(BF16)
+    near_copy(0, 1).start()
+    near_copy(1, 0).start()
     far_copy(0, 1).wait_recv()
     far_copy(1, -1).wait_recv()
     near_send[0, 0:64] = (part[0, 0:64] + far_recv[0].astype(F32)).astype(BF16)
-    near_send[0, 64:128] = part[0, 64:128].astype(BF16)
-    near_send[1, 0:64] = part[1, 0:64].astype(BF16)
     near_send[1, 64:128] = (part[1, 64:128] + far_recv[1].astype(F32)).astype(BF16)
-    near_copy(0, 1).start()
-    near_copy(1, -1).start()
 
     def wait_ctx(k):
         s = origin(k)
@@ -330,8 +350,8 @@
         s = origin(k)
         pool_copy(down_stage.at[s], pages_of(down_all, s), down_s, down_r, k, s).wait_recv()
 
-    each(0, POOL, wait_down)
-    each(0, POOL, wait_ctx)
+    each(1, POOL, wait_down)
+    each(1, POOL, wait_ctx)
 
     low = lax.broadcasted_iota(jnp.int32, (32, 128), 1) < 64
     keep = own_block((32, 256))
@@ -354,57 +374,87 @@
 
     lax.fori_loop(0, POOL, down_block, 0)
 
-    def send_z(k):
-        pool_copy(z_send.at[peer(k)], z_recv.at[me], z_s, z_r, k, peer(k)).start()
-
-    each(0, POOL, send_z)
-    z_recv[me] = z_send[me]
-    each(*BATCH[1], send_up)
-
+    def quarter_rows(ref, o):
+        return ref.at[:, pl.ds(pl.multiple_of(lax.rem(x + o, SIDE) * 16, 16), 16), :]
+
+    def line_copy(src, dst, ssem, rsem, o):
+        return pltpu.make_async_remote_copy(
+            src_ref=src,
+            dst_ref=dst,
+            send_sem=ssem.at[o - 1],
+            recv_sem=rsem.at[o - 1],
+            device_id={"tp": lax.rem(x + o, SIDE)},
+            device_id_type=MESH,
+        )
+
+    def part_copy(o):
+        return line_copy(quarter_rows(z_send, o), zx_recv.at[o - 1], zx_s, zx_r, o)
+
+    for o in (2, 1, 3):
+        part_copy(o).start()
+    near_copy(0, 0).start()
+    near_copy(1, 1).start()
     for i in range(12, 14):
         wo_tile(i)
+    for o in (1, 2, 3):
+        part_copy(o).wait_recv()
+    mine = pl.ds(pl.multiple_of(x * 16, 16), 16)
+    total = z_send[:, mine, :].astype(F32)
+    for o in range(3):
+        total = total + zx_recv[o].astype(F32)
+    zq_send[...] = total.astype(BF16)
+
+    def send_z(k):
+        pool_copy(zq_send.at[peer(k)], zq_recv.at[me], z_s, z_r, k, peer(k)).start()
+
+    for k in EVEN:
+        send_z(k)
+    zq_recv[me] = zq_send[me]
+    for k in BATCH[1]:
+        send_up(k)
+    wo_tile(14)
 
     def wait_z(k):
         s = origin(k)
-        pool_copy(z_send.at[s], z_recv.at[s], z_s, z_r, k, s).wait_recv()
-
-    each(0, POOL, wait_z)
-    total = z_recv[0].astype(F32)
+        pool_copy(zq_send.at[s], zq_recv.at[s], z_s, z_r, k, s).wait_recv()
+
+    each(1, POOL, wait_z)
+    total = zq_recv[0].astype(F32)
     for p in range(1, POOL):
-        total = total + z_recv[p].astype(F32)
-    zt_send[...] = total.astype(BF16)
-
-    def zt_copy(o):
-        return pltpu.make_async_remote_copy(
-            src_ref=zt_send,
-            dst_ref=zt_recv.at[o - 1],
-            send_sem=zt_s.at[o - 1],
-            recv_sem=zt_r.at[o - 1],
-            device_id={"tp": lax.rem(x + o, SIDE)},
-            device_id_type=MESH,
-        )
+        total = total + zq_recv[p].astype(F32)
+    z_own[...] = total.astype(BF16)
+
+    def send_za(k):
+        pool_copy(z_own, zq_all.at[me], za_s, za_r, k, peer(k)).start()
+
+    for k in EVEN:
+        send_za(k)
+    zq_all[me] = z_own[...]
+    for k in BATCH[2]:
+        send_up(k)
+    wo_tile(15)
+
+    def wait_za(k):
+        pool_copy(z_own, zq_all.at[origin(k)], za_s, za_r, k, origin(k)).wait_recv()
+
+    each(1, POOL, wait_za)
+
+    def whole_copy(o):
+        rows = z_all.at[:, mine, :]
+        return line_copy(zq_all, rows, zt_s, zt_r, o)
+
+    def whole_wait(o):
+        rows = quarter_rows(z_all, SIDE - o)
+        line_copy(zq_all, rows, zt_s, zt_r, o).wait_recv()
 
     for o in (2, 1, 3):
-        zt_copy(o).start()
-    for i in range(14, 16):
-        wo_tile(i)
-    for o in (1, 2, 3):
-        zt_copy(o).wait_recv()
-    total = zt_send[...].astype(F32)
-    for o in range(3):
-        total = total + zt_recv[o].astype(F32)
-    z_own[...] = total.astype(BF16)
-
-    def send_za(k):
-        pool_copy(z_own, z_all.at[me], za_s, za_r, k, peer(k)).start()
-
-    each(0, POOL, send_za)
-    z_all[me] = z_own[...]
-    each(*BATCH[2], send_up)
+        whole_copy(o).start()
+    z_all[:, mine, :] = zq_all[...]
 
     hidden_copy.wait()
-    near_copy(0, 1).wait_recv()
-    near_copy(1, -1).wait_recv()
+    for i in range(2):
+        for half in range(2):
+            near_copy(i, half).wait_recv()
     own[...] = (
         own[...]
         + hidden[...].astype(F32)
@@ -412,15 +462,13 @@
         + near_recv[1].astype(F32)
     )
 
-    def wait_za(k):
-        pool_copy(z_own, z_all.at[origin(k)], za_s, za_r, k, origin(k)).wait_recv()
-
     def wait_up(k):
         s = origin(k)
         pool_copy(up_stage.at[s], pages_of(up_all, s), up_s, up_r, k, s).wait_recv()
 
-    each(0, POOL, wait_za)
-    each(0, POOL, wait_up)
+    for o in (1, 2, 3):
+        whole_wait(o)
+    each(1, POOL, wait_up)
 
     def up_block(p):
         pieces = [None] * 4
@@ -443,7 +491,7 @@
         up_block(peer(k))
         delta_copy(k, me, peer(k)).start()
 
-    each(0, POOL, up_and_send)
+    each(1, POOL, up_and_send)
     up_block(me)
     delta_recv[me] = delta_send[me]
 
@@ -451,45 +499,53 @@
         s = origin(k)
         delta_copy(k, s, s).wait_recv()
 
-    each(0, POOL, wait_delta)
-
-    def hand_copy(h):
-        rows = pl.ds(h * 64, 64)
+    def hand_copy(j):
         return pltpu.make_async_remote_copy(
-            src_ref=final.at[rows],
-            dst_ref=out_ref.at[rows],
-            send_sem=sec_s.at[h],
-            recv_sem=sec_r.at[h],
+            src_ref=final.at[j],
+            dst_ref=out_ref.at[:, pl.ds(pl.multiple_of(j * HEAD, HEAD), HEAD)],
+            send_sem=sec_s.at[j],
+            recv_sem=sec_r.at[j],
             device_id={"section": 1 - sec},
             device_id_type=MESH,
         )
 
-    for h in range(2):
-        rows = slice(h * 64, (h + 1) * 64)
-        for j in range(POOL):
-            cols = slice(j * HEAD, (j + 1) * HEAD)
-            final[rows, cols] = (own[rows, cols] + delta_recv[j, rows].astype(F32)).astype(BF16)
-        hand_copy(h).start()
+    def finish(j):
+        value = own[:, pl.ds(pl.multiple_of(j * HEAD, HEAD), HEAD)]
+        final[j] = (value + delta_recv[j].astype(F32)).astype(BF16)
+        hand_copy(j).start()
+
+    finish(me)
+
+    def take(k):
+        wait_delta(k)
+        finish(origin(k))
+
+    each(1, POOL, take)
 
     def drain(k):
         j = peer(k)
         pool_copy(down_stage.at[j], pages_of(down_all, me), down_s, down_r, k, j).wait_send()
         pool_copy(up_stage.at[j], pages_of(up_all, me), up_s, up_r, k, j).wait_send()
         pool_copy(heads.at[j], ctx_all.at[me], ctx_s, ctx_r, k, j).wait_send()
-        pool_copy(z_send.at[j], z_recv.at[me], z_s, z_r, k, j).wait_send()
-        pool_copy(z_own, z_all.at[me], za_s, za_r, k, j).wait_send()
+        pool_copy(zq_send.at[j], zq_recv.at[me], z_s, z_r, k, j).wait_send()
+        pool_copy(z_own, zq_all.at[me], za_s, za_r, k, j).wait_send()
         delta_copy(k, me, j).wait_send()
 
-    each(0, POOL, drain)
+    each(1, POOL, drain)
     for o in (1, 2, 3):
-        zt_copy(o).wait_send()
+        part_copy(o).wait_send()
+        whole_copy(o).wait_send()
     far_copy(0, 1).wait_send()
     far_copy(1, -1).wait_send()
-    near_copy(0, 1).wait_send()
-    near_copy(1, -1).wait_send()
-    for h in range(2):
-        hand_copy(h).wait_send()
-        hand_copy(h).wait_recv()
+    for i in range(2):
+        for half in range(2):
+            near_copy(i, half).wait_send()
+
+    def handed(j):
+        hand_copy(j).wait_send()
+        hand_copy(j).wait_recv()
+
+    each(0, POOL, handed)
 
 
 def per_device(
@@ -505,11 +561,8 @@
     adapter_down,
     adapter_up,
 ):
-    requests, window, head_count, head_size = queries.shape[2:]
-    rows = requests * window
+    rows = queries.shape[2] * queries.shape[3]
     width = hidden.shape[3]
-    q = queries[0, 0].transpose(0, 2, 1, 3)
-    q = q.reshape(requests, 2, head_count // 2 * window, head_size)
     pages = adapter_down.shape[:2] + (HEAD,)
     smem = pl.BlockSpec(memory_space=pltpu.SMEM)
     vmem = pl.BlockSpec(memory_space=pltpu.VMEM)
@@ -518,10 +571,11 @@
     handed = pl.pallas_call(
         kernel,
         out_shape=jax.ShapeDtypeStruct((rows, width), BF16),
-        in_specs=[smem, smem, smem, smem, vmem, hbm, hbm, hbm, hbm, hbm, hbm],
+        in_specs=[smem, smem, smem, smem, hbm, hbm, hbm, hbm, hbm, hbm, hbm],
         out_specs=vmem,
         scratch_shapes=[
             pltpu.VMEM(cached_key_value.shape[2:], BF16),
+            pltpu.VMEM(queries.shape[2:], BF16),
             pltpu.VMEM(window_key_value.shape[2:], BF16),
             pltpu.VMEM((rows, width), BF16),
             pltpu.VMEM((POOL,) + pages, BF16),
@@ -540,14 +594,15 @@
             pltpu.VMEM((2, rows, width), BF16),
             pltpu.VMEM((rows, width), F32),
             pltpu.VMEM((POOL, 64, HEAD), BF16),
-            pltpu.VMEM((POOL, 64, HEAD), BF16),
-            pltpu.VMEM((64, HEAD), BF16),
-            pltpu.VMEM((3, 64, HEAD), BF16),
-            pltpu.VMEM((64, HEAD), BF16),
+            pltpu.VMEM((3, POOL, 16, HEAD), BF16),
+            pltpu.VMEM((POOL, 16, HEAD), BF16),
+            pltpu.VMEM((POOL, 16, HEAD), BF16),
+            pltpu.VMEM((16, HEAD), BF16),
+            pltpu.VMEM((POOL, 16, HEAD), BF16),
             pltpu.VMEM((POOL, 64, HEAD), BF16),
             pltpu.VMEM((POOL, rows, HEAD), BF16),
             pltpu.VMEM((POOL, rows, HEAD), BF16),
-            pltpu.VMEM((rows, width), BF16),
+            pltpu.VMEM((POOL, rows, HEAD), BF16),
             dma((40,)),
             dma((BUFS,)),
             dma((POOL,)),
@@ -562,12 +617,14 @@
             dma((POOL,)),
             dma((POOL,)),
             dma((POOL,)),
-            dma((4,)),
-            dma((4,)),
+            dma((6,)),
+            dma((6,)),
             dma((3,)),
             dma((3,)),
-            dma((2,)),
-            dma((2,)),
+            dma((3,)),
+            dma((3,)),
+            dma((POOL,)),
+            dma((POOL,)),
         ],
         compiler_params=pltpu.CompilerParams(
             collective_id=0, has_side_effects=True, vmem_limit_bytes=60 * 2**20
@@ -578,7 +635,7 @@
         request_page_table,
         request_adapter,
         layer_page_slot,
-        q,
+        queries,
         window_key_value,
         cached_key_value,
         adapter_down,

time: 101 us -> 87.5 us (0.87)
  Pallas kernels: 97.2 us -> 85.4 us
  local copies, waits for them, and re-layouts: 3.85 us -> 1.88 us
    pallas_call x1, Pallas kernels: 97.2 us -> 85.4 us  [per_device(): pl.pallas_call(kernel, out_shape=jax.ShapeDtypeStruct((rows, width), BF16...]
    transpose x1 -> x0, local copies, waits for them, and re-layouts: 1.97 us -> none  [per_device(): q = queries[0, 0].transpose(0, 2, 1, 3)]
where the time goes in v3:
time: 87.5 us; the launch traced here: 87.3 us
  Pallas kernels  85.4 us (98%)
  local copies, waits for them, and re-layouts  1.88 us (2%)
    pallas_call x1, Pallas kernels, per_device(): pl.pallas_call(kernel, out_shape=jax.ShapeDtypeStruct((rows, width), BF16...  85.4 us
    unnamed x1, local copies, waits for them, and re-layouts  1.88 us

profile of v3, /device:TPU:1, one launch (start us, length us, event | category | flops | bytes accessed | tf_op | source)
XLA Modules:
  0.0 87.3 jit_solution(15590965008341885712)
XLA Ops:
  0.0 85.4 %relay_layer.1 = bf16[128,2048]{1,0:T(8,128)(2,1)} custom-call(s32[1,1,16]{2,1,0:T(1,128)} %len_ref.1, s32[1,1,16,16]{3,2,1,0:T(8,128)} %table_ref.1, s32[2,16,16]{2,1,0:T(8,128)} %adapter_ref.1, s32[256]{0:T(256)} %layer_ref.1, bf16[1,1,16,8,16,128]{5,4,3,2,1,0:T(8,128)(2,1)} %q_hbm.1, bf16[1,1,16,2,2,8,128]{6,5,4,3,2,1,0:T(8,128)(2,1)} %wkv_hbm.1, ...), custom_call_target="tpu_custom_call" | custom-call | tf_op jit(solution)/shard_map/relay_layer/pallas_call | solution.py:571
  85.4 1.9 %copy.13 = bf16[1,1,128,2048]{3,2,1,0:T(8,128)(2,1)} copy(bf16[1,1,128,2048]{3,2,1,0:T(8,128)(2,1)} %bitcast.1) | data formatting | bytes 1048576

commit v4 on v3

--- a/solution.py
+++ b/solution.py
@@ -10,7 +10,6 @@
 F32 = jnp.float32
 BF16 = jnp.bfloat16
 NT = (((1,), (1,)), ((), ()))
-TN = (((0,), (0,)), ((), ()))
 MESH = pl.DeviceIdType.MESH
 SIDE = 4
 POOL = SIDE * SIDE
@@ -23,7 +22,8 @@
     (1, 2), (3, 2), (2, 0), (0, 1), (0, 3),
 )
 EVEN = tuple(dz + SIDE * ((dy - dz) % SIDE) for dz, dy in OFFSETS)
-BATCH = (EVEN[:7], EVEN[7:11], EVEN[11:])
+BATCH = (EVEN[:5], EVEN[5:], (), ())
+ORDER = (2, 1, 3, 0)
 
 
 def own_block(shape):
@@ -63,22 +63,22 @@
             axis=0,
         )
 
-    s = lax.dot_general(side(0), query, NT, preferred_element_type=F32) * scale
-    position = lax.broadcasted_iota(jnp.int32, s.shape, 0)
+    s = lax.dot_general(query, side(0), NT, preferred_element_type=F32) * scale
+    position = lax.broadcasted_iota(jnp.int32, s.shape, 1)
     s = jnp.where(position < length, s, -1e30)
-    sw = lax.dot_general(window_key, query, NT, preferred_element_type=F32) * scale
-    row = lax.broadcasted_iota(jnp.int32, sw.shape, 0)
-    token = lax.broadcasted_iota(jnp.int32, sw.shape, 1) % 8
-    sw = jnp.where(row <= token, sw, -1e30)
-    top = jnp.maximum(jnp.max(s, axis=0, keepdims=True), jnp.max(sw, axis=0, keepdims=True))
+    sw = lax.dot_general(query, window_key, NT, preferred_element_type=F32) * scale
+    token = lax.broadcasted_iota(jnp.int32, sw.shape, 0) % 8
+    place = lax.broadcasted_iota(jnp.int32, sw.shape, 1)
+    sw = jnp.where(place <= token, sw, -1e30)
+    top = jnp.maximum(jnp.max(s, axis=1, keepdims=True), jnp.max(sw, axis=1, keepdims=True))
     p = jnp.exp(s - top)
     pw = jnp.exp(sw - top)
-    total = jnp.sum(p, axis=0, keepdims=True) + jnp.sum(pw, axis=0, keepdims=True)
+    total = jnp.sum(p, axis=1, keepdims=True) + jnp.sum(pw, axis=1, keepdims=True)
     inverse = 1.0 / total
     p = (p * inverse).astype(BF16)
     pw = (pw * inverse).astype(BF16)
-    out = lax.dot_general(p, side(1), TN, preferred_element_type=F32)
-    out = out + lax.dot_general(pw, window_value, TN, preferred_element_type=F32)
+    out = jnp.dot(p, side(1), preferred_element_type=F32)
+    out = out + jnp.dot(pw, window_value, preferred_element_type=F32)
     rows = pl.ds(pl.multiple_of(r * 8, 8), 8)
     ctx32[0:8, rows, :] = out[0:64, 0:128].reshape(8, 8, 128)
     ctx32[8:16, rows, :] = out[64:128, 128:256].reshape(8, 8, 128)
@@ -187,6 +187,16 @@
             device_id_type=MESH,
         )
 
+    def next_copy(src, dst, ssem, rsem, k, to):
+        return pltpu.make_async_remote_copy(
+            src_ref=src,
+            dst_ref=dst,
+            send_sem=ssem.at[k],
+            recv_sem=rsem.at[k],
+            device_id={"pool": to, "tp": lax.rem(x + 1, SIDE)},
+            device_id_type=MESH,
+        )
+
     def columns(ref, j):
         return ref.at[:, :, pl.ds(pl.multiple_of(j * HEAD, HEAD), HEAD)]
 
@@ -226,13 +236,19 @@
     def greet(k):
         pl.semaphore_signal(barrier, inc=1, device_id={"pool": peer(k)}, device_id_type=MESH)
 
+    def greet_behind(k):
+        before = lax.rem(x + 3, SIDE)
+        target = {"pool": peer(k), "tp": before}
+        pl.semaphore_signal(barrier, inc=1, device_id=target, device_id_type=MESH)
+
     each(1, POOL, greet)
+    each(1, POOL, greet_behind)
     for o in (1, 2, 3):
         pl.semaphore_signal(
             barrier, inc=1, device_id={"tp": lax.rem(x + o, SIDE)}, device_id_type=MESH
         )
     pl.semaphore_signal(barrier, inc=1, device_id={"section": 1 - sec}, device_id_type=MESH)
-    pl.semaphore_wait(barrier, POOL - 1 + 3 + 1)
+    pl.semaphore_wait(barrier, 2 * (POOL - 1) + 3 + 1)
     for i in range(4):
         cache_copy(i).start()
 
@@ -255,7 +271,7 @@
     hidden_copy.start()
 
     def wo_copy(i):
-        target = lax.rem(x + (2, 1, 3, 0)[i // 4], SIDE)
+        target = lax.rem(x + ORDER[i // 4], SIDE)
         col = target * (SIDE * TILE) + (i % 4) * TILE
         return pltpu.make_async_copy(
             wo_hbm.at[0, :, pl.ds(pl.multiple_of(col, TILE), TILE)],
@@ -283,8 +299,7 @@
     def send_ctx(k):
         pool_copy(heads.at[peer(k)], ctx_all.at[me], ctx_s, ctx_r, k, peer(k)).start()
 
-    for k in EVEN:
-        send_ctx(k)
+    each(1, POOL, send_ctx)
     ctx_all[me] = heads[me]
 
     def send_up(k):
@@ -331,16 +346,10 @@
         wo_tile(i)
     far_copy(0, 1).start()
     far_copy(1, -1).start()
-    for i in range(4, 12):
+    for i in range(4, 8):
         wo_tile(i)
     near_send[0, 64:128] = part[0, 64:128].astype(BF16)
-    near_send[1, 0:64] = part[1, 0:64].astype(BF16)
     near_copy(0, 1).start()
-    near_copy(1, 0).start()
-    far_copy(0, 1).wait_recv()
-    far_copy(1, -1).wait_recv()
-    near_send[0, 0:64] = (part[0, 0:64] + far_recv[0].astype(F32)).astype(BF16)
-    near_send[1, 64:128] = (part[1, 64:128] + far_recv[1].astype(F32)).astype(BF16)
 
     def wait_ctx(k):
         s = origin(k)
@@ -351,7 +360,6 @@
         pool_copy(down_stage.at[s], pages_of(down_all, s), down_s, down_r, k, s).wait_recv()
 
     each(1, POOL, wait_down)
-    each(1, POOL, wait_ctx)
 
     low = lax.broadcasted_iota(jnp.int32, (32, 128), 1) < 64
     keep = own_block((32, 256))
@@ -359,7 +367,7 @@
     def gathered(ref, p, g):
         return jnp.concatenate([ref[slot(p, g * 4 + a)] for a in range(4)], axis=0)
 
-    def down_block(p, carry):
+    def down_block(p):
         pieces = []
         for g in range(4):
             pages = gathered(down_all, p, g)
@@ -370,9 +378,17 @@
             pieces.append(half + pltpu.roll(half, 64, 1))
         z_send[p, 0:32, :] = jnp.where(low, pieces[0], pieces[2]).astype(BF16)
         z_send[p, 32:64, :] = jnp.where(low, pieces[1], pieces[3]).astype(BF16)
-        return carry
-
-    lax.fori_loop(0, POOL, down_block, 0)
+
+
+    for k in BATCH[1]:
+        send_up(k)
+    down_block(me)
+
+    def arrived(k):
+        wait_ctx(k)
+        down_block(origin(k))
+
+    each(1, POOL, arrived)
 
     def quarter_rows(ref, o):
         return ref.at[:, pl.ds(pl.multiple_of(lax.rem(x + o, SIDE) * 16, 16), 16), :]
@@ -392,9 +408,7 @@
 
     for o in (2, 1, 3):
         part_copy(o).start()
-    near_copy(0, 0).start()
-    near_copy(1, 1).start()
-    for i in range(12, 14):
+    for i in range(8, 10):
         wo_tile(i)
     for o in (1, 2, 3):
         part_copy(o).wait_recv()
@@ -405,62 +419,63 @@
     zq_send[...] = total.astype(BF16)
 
     def send_z(k):
-        pool_copy(zq_send.at[peer(k)], zq_recv.at[me], z_s, z_r, k, peer(k)).start()
-
-    for k in EVEN:
+        next_copy(zq_send.at[peer(k)], zq_recv.at[me], z_s, z_r, k, peer(k)).start()
+
+    for k in EVEN + (0,):
         send_z(k)
-    zq_recv[me] = zq_send[me]
-    for k in BATCH[1]:
+    for k in BATCH[2]:
         send_up(k)
-    wo_tile(14)
+    for i in range(10, 12):
+        wo_tile(i)
+    near_send[1, 0:64] = part[1, 0:64].astype(BF16)
+    near_copy(1, 0).start()
 
     def wait_z(k):
         s = origin(k)
-        pool_copy(zq_send.at[s], zq_recv.at[s], z_s, z_r, k, s).wait_recv()
-
-    each(1, POOL, wait_z)
+        next_copy(zq_send.at[s], zq_recv.at[s], z_s, z_r, k, s).wait_recv()
+
+    each(0, POOL, wait_z)
     total = zq_recv[0].astype(F32)
     for p in range(1, POOL):
         total = total + zq_recv[p].astype(F32)
     z_own[...] = total.astype(BF16)
 
     def send_za(k):
-        pool_copy(z_own, zq_all.at[me], za_s, za_r, k, peer(k)).start()
-
-    for k in EVEN:
+        next_copy(z_own, zq_all.at[me], za_s, za_r, k, peer(k)).start()
+
+    for k in EVEN + (0,):
         send_za(k)
-    zq_all[me] = z_own[...]
-    for k in BATCH[2]:
+    for k in BATCH[3]:
         send_up(k)
-    wo_tile(15)
+    for i in range(12, 14):
+        wo_tile(i)
+    far_copy(0, 1).wait_recv()
+    far_copy(1, -1).wait_recv()
+    near_send[0, 0:64] = (part[0, 0:64] + far_recv[0].astype(F32)).astype(BF16)
+    near_send[1, 64:128] = (part[1, 64:128] + far_recv[1].astype(F32)).astype(BF16)
 
     def wait_za(k):
-        pool_copy(z_own, zq_all.at[origin(k)], za_s, za_r, k, origin(k)).wait_recv()
-
-    each(1, POOL, wait_za)
+        next_copy(z_own, zq_all.at[origin(k)], za_s, za_r, k, origin(k)).wait_recv()
+
+    each(0, POOL, wait_za)
 
     def whole_copy(o):
-        rows = z_all.at[:, mine, :]
+        rows = quarter_rows(z_all, 2)
         return line_copy(zq_all, rows, zt_s, zt_r, o)
 
     def whole_wait(o):
-        rows = quarter_rows(z_all, SIDE - o)
+        rows = quarter_rows(z_all, SIDE - o + 2)
         line_copy(zq_all, rows, zt_s, zt_r, o).wait_recv()
 
     for o in (2, 1, 3):
         whole_copy(o).start()
-    z_all[:, mine, :] = zq_all[...]
-
-    hidden_copy.wait()
-    for i in range(2):
-        for half in range(2):
-            near_copy(i, half).wait_recv()
-    own[...] = (
-        own[...]
-        + hidden[...].astype(F32)
-        + near_recv[0].astype(F32)
-        + near_recv[1].astype(F32)
-    )
+    held_rows = pl.ds(pl.multiple_of(lax.rem(x + 2, SIDE) * 16, 16), 16)
+    z_all[:, held_rows, :] = zq_all[...]
+
+    near_copy(0, 0).start()
+    near_copy(1, 1).start()
+    for i in range(14, 16):
+        wo_tile(i)
 
     def wait_up(k):
         s = origin(k)
@@ -494,6 +509,17 @@
     each(1, POOL, up_and_send)
     up_block(me)
     delta_recv[me] = delta_send[me]
+    hidden_copy.wait()
+    for i in range(2):
+        for half in range(2):
+            near_copy(i, half).wait_recv()
+    own[...] = (
+        own[...]
+        + hidden[...].astype(F32)
+        + near_recv[0].astype(F32)
+        + near_recv[1].astype(F32)
+    )
+
 
     def wait_delta(k):
         s = origin(k)
@@ -527,11 +553,15 @@
         pool_copy(down_stage.at[j], pages_of(down_all, me), down_s, down_r, k, j).wait_send()
         pool_copy(up_stage.at[j], pages_of(up_all, me), up_s, up_r, k, j).wait_send()
         pool_copy(heads.at[j], ctx_all.at[me], ctx_s, ctx_r, k, j).wait_send()
-        pool_copy(zq_send.at[j], zq_recv.at[me], z_s, z_r, k, j).wait_send()
-        pool_copy(z_own, zq_all.at[me], za_s, za_r, k, j).wait_send()
         delta_copy(k, me, j).wait_send()
 
+    def drain_z(k):
+        j = peer(k)
+        next_copy(zq_send.at[j], zq_recv.at[me], z_s, z_r, k, j).wait_send()
+        next_copy(z_own, zq_all.at[me], za_s, za_r, k, j).wait_send()
+
     each(1, POOL, drain)
+    each(0, POOL, drain_z)
     for o in (1, 2, 3):
         part_copy(o).wait_send()
         whole_copy(o).wait_send()

time: 87.5 us -> 85.3 us (0.975)
  Pallas kernels: 85.4 us -> 83.2 us
    pallas_call x1, Pallas kernels: 85.4 us -> 83.2 us  [per_device(): pl.pallas_call(kernel, out_shape=jax.ShapeDtypeStruct((rows, width), BF16...]
where the time goes in v4:
time: 85.3 us; the launch traced here: 85.1 us
  Pallas kernels  83.2 us (98%)
  local copies, waits for them, and re-layouts  1.88 us (2%)
    pallas_call x1, Pallas kernels, per_device(): pl.pallas_call(kernel, out_shape=jax.ShapeDtypeStruct((rows, width), BF16...  83.2 us
    unnamed x1, local copies, waits for them, and re-layouts  1.88 us

profile of v4, /device:TPU:1, one launch (start us, length us, event | category | flops | bytes accessed | tf_op | source)
XLA Modules:
  0.0 85.1 jit_solution(3879783936594067230)
XLA Ops:
  0.0 83.2 %relay_layer.1 = bf16[128,2048]{1,0:T(8,128)(2,1)} custom-call(s32[1,1,16]{2,1,0:T(1,128)} %len_ref.1, s32[1,1,16,16]{3,2,1,0:T(8,128)} %table_ref.1, s32[2,16,16]{2,1,0:T(8,128)} %adapter_ref.1, s32[256]{0:T(256)} %layer_ref.1, bf16[1,1,16,8,16,128]{5,4,3,2,1,0:T(8,128)(2,1)} %q_hbm.1, bf16[1,1,16,2,2,8,128]{6,5,4,3,2,1,0:T(8,128)(2,1)} %wkv_hbm.1, ...), custom_call_target="tpu_custom_call" | custom-call | tf_op jit(solution)/shard_map/relay_layer/pallas_call | solution.py:601
  83.2 1.9 %copy.13 = bf16[1,1,128,2048]{3,2,1,0:T(8,128)(2,1)} copy(bf16[1,1,128,2048]{3,2,1,0:T(8,128)(2,1)} %bitcast.1) | data formatting | bytes 1048576
